TPU v7x, 128 devices: a whole 4x4x4 slice. The times are simulated.
128 devices in a mesh: dp: 4 (over z), seq: 8 (over y_lo, x), tensor: 4 (over y_hi, core).
Axes of the slice: x: 4, y: 4 (y_hi: 2, y_lo: 2; y = y_hi * 2 + y_lo), z: 4, core: 2. Of those that a mesh axis runs over, the one named last changes fastest.
Arguments:
- hidden_in: bfloat16 [65536, 2880], P(('dp', 'seq', 'tensor')), parts along dimension 0, may hold values from -6 to 6
- norm_gain: float32 [2880], replicated, may hold values from 0.5 to 1.5
- conv_weight: float32 [4, 2880], replicated, may hold values from -3 to 3
- w_query: bfloat16 [2880, 2048], P(None, 'tensor'), may hold values from -32 to 32
- w_key: bfloat16 [2880, 512], P(None, 'tensor'), may hold values from -1 to 1
- w_value: bfloat16 [2880, 512], P(None, 'tensor'), may hold values from -0.109375 to 0.109375
- w_out: bfloat16 [2048, 2880], P('tensor'), may hold values from -0.125 to 0.125
- doc_ids: int32 [65536], P(('dp', 'seq')), parts along dimension 0, may hold values from 0 to 63, never falling along the last dimension, each value on 1 to 1024 neighbouring positions
Outputs:
- hidden_out: bfloat16 [65536, 2880], P(('dp', 'seq', 'tensor')), parts along dimension 0
There are 4 independent parts, one for each index of `dp`. A program takes and returns all parts, laid end to end along the dimension named above; an argument that names none is the same for every part. Nothing has to cross between parts.
Inputs may be any that keep to these rules, and one draw needn't show every extreme that they name: `doc_ids`: document numbers never fall along a window's tokens.
All inputs are finite; a program needn't handle non-finite values.
Results may differ from a plain program's by a relative error of at most 0.011.
Values may be sent and summed in bfloat16 or wider, within the bound.
A program may use at most 128 MiB of HBM per device.

v0:
```python
import math

import jax
import jax.numpy as jnp
from jax import lax
from jax.sharding import PartitionSpec as P

HEAD = 64
WINDOW = 128
QBLOCK = 512


eps = 1e-05
rope_base = 150000.0


def passed_along(array, axis, by):
    devices = lax.axis_size(axis)
    pairs = [(i, i + by) for i in range(devices) if 0 <= i + by < devices]
    return lax.ppermute(array, axis, pairs)


def rotate(values, positions):
    rows = values.shape[0]
    half = HEAD // 2
    frequency = jnp.exp(jnp.arange(half, dtype=jnp.float32) * (-2.0 * math.log(rope_base) / HEAD))
    angle = positions.astype(jnp.float32)[:, None] * frequency[None, :]
    cosine = jnp.cos(angle)[:, None, :]
    sine = jnp.sin(angle)[:, None, :]
    shaped = values.reshape(rows, -1, HEAD)
    first = shaped[:, :, :half]
    second = shaped[:, :, half:]
    turned = jnp.concatenate(
        [first * cosine - second * sine, second * cosine + first * sine], axis=2
    )
    return turned.reshape(rows, -1)


def attend(queries, keys, values, query_pos, key_pos, query_doc, key_doc):
    scores = jnp.einsum("qhgd,khd->hgqk", queries, keys, preferred_element_type=jnp.float32) * (
        1.0 / math.sqrt(HEAD)
    )
    visible = (key_pos[None, :] <= query_pos[:, None]) & (
        key_pos[None, :] > query_pos[:, None] - WINDOW
    )
    visible = visible & (key_pos[None, :] >= 0) & (key_doc[None, :] == query_doc[:, None])
    scores = jnp.where(visible[None, None, :, :], scores, -jnp.inf)
    largest = jnp.max(scores, axis=3, keepdims=True)
    weights = jnp.exp(scores - largest)
    total = jnp.sum(weights, axis=3)
    rounded = weights.astype(jnp.bfloat16)
    summed = jnp.einsum("hgqk,khd->qhgd", rounded, values, preferred_element_type=jnp.float32)
    result = summed / jnp.transpose(total, (2, 0, 1))[:, :, :, None]
    return result.reshape(result.shape[0], -1).astype(jnp.bfloat16)


def local(hidden_in, norm_gain, conv_weight, w_query, w_key, w_value, w_out, doc_ids):
    rows = hidden_in.shape[0]
    width = hidden_in.shape[1]
    taps = conv_weight.shape[0]
    inputs = hidden_in.astype(jnp.float32)
    mean_square = jnp.mean(inputs * inputs, axis=1, keepdims=True)
    normed = (inputs * lax.rsqrt(mean_square + eps) * norm_gain[None, :]).astype(jnp.bfloat16)
    earlier = passed_along(normed[rows - (taps - 1) :], ("seq", "tensor"), 1)
    extended = jnp.concatenate([earlier, normed], axis=0).astype(jnp.float32)
    convolved = jnp.zeros((rows, width), jnp.float32)
    for tap in range(taps):
        convolved = (
            convolved + conv_weight[tap][None, :] * extended[taps - 1 - tap : taps - 1 - tap + rows]
        )
    mixed = convolved.astype(jnp.bfloat16)
    query_cols = w_query.shape[1]
    key_cols = w_key.shape[1]
    piece = lax.all_gather(mixed, "tensor", axis=0, tiled=True)
    projected = jnp.concatenate(
        [
            jnp.dot(piece, w_query, preferred_element_type=jnp.float32),
            jnp.dot(piece, w_key, preferred_element_type=jnp.float32),
            jnp.dot(piece, w_value, preferred_element_type=jnp.float32),
        ],
        axis=1,
    )
    span = projected.shape[0]
    offset = lax.axis_index("seq") * span
    positions = offset + jnp.arange(span, dtype=jnp.int32)
    queries = rotate(projected[:, :query_cols], positions).astype(jnp.bfloat16)
    keys = rotate(projected[:, query_cols : query_cols + key_cols], positions).astype(jnp.bfloat16)
    values = projected[:, query_cols + key_cols :].astype(jnp.bfloat16)
    key_rim, value_rim = passed_along((keys[span - WINDOW :], values[span - WINDOW :]), "seq", 1)
    doc_rim = passed_along(doc_ids[span - WINDOW :], "seq", 1)
    heads_here = query_cols // HEAD
    kv_here = key_cols // HEAD
    groups = heads_here // kv_here
    query_four = queries.reshape(span, kv_here, groups, HEAD)
    key_ext = jnp.concatenate([key_rim, keys], axis=0).reshape(span + WINDOW, kv_here, HEAD)
    value_ext = jnp.concatenate([value_rim, values], axis=0).reshape(span + WINDOW, kv_here, HEAD)
    doc_ext = jnp.concatenate([doc_rim, doc_ids], axis=0)
    pos_ext = offset - WINDOW + jnp.arange(span + WINDOW, dtype=jnp.int32)

    def one_block(index):
        begin = index * QBLOCK
        block_q = lax.dynamic_slice_in_dim(query_four, begin, QBLOCK, 0)
        block_k = lax.dynamic_slice_in_dim(key_ext, begin, QBLOCK + WINDOW, 0)
        block_v = lax.dynamic_slice_in_dim(value_ext, begin, QBLOCK + WINDOW, 0)
        query_pos = lax.dynamic_slice_in_dim(positions, begin, QBLOCK, 0)
        key_pos = lax.dynamic_slice_in_dim(pos_ext, begin, QBLOCK + WINDOW, 0)
        query_doc = lax.dynamic_slice_in_dim(doc_ids, begin, QBLOCK, 0)
        key_doc = lax.dynamic_slice_in_dim(doc_ext, begin, QBLOCK + WINDOW, 0)
        return attend(block_q, block_k, block_v, query_pos, key_pos, query_doc, key_doc)

    blocks = lax.map(one_block, jnp.arange(span // QBLOCK, dtype=jnp.int32))
    attended = blocks.reshape(span, query_cols)
    regrouped = lax.all_to_all(attended, "tensor", split_axis=0, concat_axis=1, tiled=True)
    summed = jnp.dot(
        regrouped,
        lax.all_gather(w_out, "tensor", axis=0, tiled=True),
        preferred_element_type=jnp.float32,
    )
    return (inputs + summed).astype(jnp.bfloat16)


def solution(mesh):
    in_specs = (
        P(("dp", "seq", "tensor"), None),
        P(),
        P(),
        P(None, "tensor"),
        P(None, "tensor"),
        P(None, "tensor"),
        P("tensor", None),
        P(("dp", "seq")),
    )
    out_specs = P(("dp", "seq", "tensor"), None)
    return jax.shard_map(local, mesh=mesh, in_specs=in_specs, out_specs=out_specs, check_vma=False)
```

profile of v0, /device:TPU:1, one launch (start us, length us, event | category | flops | bytes accessed | tf_op | source)
XLA Modules:
  0.0 245.1 jit_solution(8383552326062638265)
XLA Ops:
  6.5 2.7 %fusion.21 = f32[512]{0:T(512)S(1)} fusion(bf16[512,2880]{0,1:T(8,128)(2,1)} %param.10), kind=kLoop, calls=%fused_computation.26 | loop fusion | flops 4423168 | bytes 2951168 | tf_op jit(solution)/shard_map/reduce_sum | solution.py:62
  9.2 2.5 %fusion.23 = bf16[512,2880]{0,1:T(8,128)(2,1)S(1)} fusion(bf16[512,2880]{0,1:T(8,128)(2,1)} %param.10, f32[2880]{0:T(1024)} %param.11, f32[512]{0:T(512)S(1)} %add_rsqrt_fusion), kind=kLoop, calls=%fused_computation.28 | loop fusion | flops 5898240 | bytes 5911808 | tf_op jit(solution)/shard_map/convert_element_type | solution.py:63
  11.8 1.6 copy-done.2
  13.4 1.1 slice.68
  14.5 1.4 copy.14
  15.9 6.2 %collective-permute-start = (bf16[3,2880]{1,0:T(4,128)(2,1)S(1)}, bf16[3,2880]{1,0:T(4,128)(2,1)S(1)}, u32[]{:S(2)}, u32[]{:S(2)}) collective-permute-start(bf16[3,2880]{1,0:T(4,128)(2,1)S(1)} %copy.14), channel_id=1, source_target_pairs={{0,1},{1,2},{2,3},{3,4},{4,5},{5,6},{6,7},{7,8},{8,9},{9,10},{10,1... | collective-permute-start | bytes 51848 | tf_op jit(solution)/shard_map/ppermute | solution.py:20
  22.3 0.8 collective-permute-done
  23.0 1.2 copy.15
  24.2 3.7 %maximum_convert_fusion = f32[515,2880]{0,1:T(8,128)S(1)} fusion(bf16[512,2880]{0,1:T(8,128)(2,1)} %copy-done.2, bf16[3,2880]{0,1:T(8,128)(2,1)} %copy.15), kind=kLoop, calls=%fused_computation.38 | loop fusion | flops 5932800 | bytes 8899200 | tf_op jit(solution)/shard_map/convert_element_type | solution.py:65
  27.9 8.3 %fusion.26 = bf16[512,2880]{0,1:T(8,128)(2,1)} fusion(f32[515,2880]{0,1:T(8,128)S(1)} %maximum_convert_fusion, f32[2880]{0:T(1024)S(1)} %get-tuple-element.143, f32[2880]{0:T(1024)S(1)} %get-tuple-element.144, f32[2880]{0:T(1024)S(1)} %get-tuple-element.142, f32[2880]{0:T(1024)S(1)} %get-tuple-element.141), kind=kLoop, calls=%fused_computation.32 | loop fusion | flops 11796480 | bytes 26588160 | tf_op jit(solution)/shard_map/convert_element_type | solution.py:71
  36.3 3.1 %collective-permute-start.2 = (s32[128]{0:T(128)S(1)}, s32[128]{0:T(128)S(1)}, u32[]{:S(2)}, u32[]{:S(2)}) collective-permute-start(s32[128]{0:T(128)S(1)} %slice.61), channel_id=1, source_target_pairs={{0,4},{4,8},{8,12},{12,16},{16,20},{20,24},{24,28},{1,5},{5,9},{9,... | collective-permute-start | bytes 1544 | tf_op jit(solution)/shard_map/ppermute | solution.py:20
  39.5 1.0 multiply_cosine_fusion
  40.5 80.6 %all-gather.3.cloned.1.call-done = bf16[2048,2880]{0,1:T(8,128)(2,1)} async-done(((bf16[512,2880]{0,1:T(8,128)(2,1)}), bf16[2048,2880]{0,1:T(8,128)(2,1)}) %all-gather.3.cloned.1.call-update) | async-done | bytes 11796496 | tf_op jit(solution)/shard_map/all_gather | solution.py:74
  121.2 6.5 %fusion.31 = f32[2048,128]{0,1:T(8,128)S(1)} fusion(bf16[2048,2880]{0,1:T(8,128)(2,1)} %all-gather.3.cloned.1.call-done, bf16[2880,128]{1,0:T(8,128)(2,1)} %param.14), kind=kOutput, calls=%fused_computation.63 | convolution fusion | flops 1509949440 | bytes 13582336 | tf_op jit(solution)/shard_map/dot_general | solution.py:78
  127.8 0.6 fusion.29
  128.4 3.3 %collective-permute-start.3 = (bf16[128,128]{0,1:T(8,128)(2,1)}, bf16[128,128]{0,1:T(8,128)(2,1)S(1)}, u32[]{:S(2)}, u32[]{:S(2)}) collective-permute-start(bf16[128,128]{0,1:T(8,128)(2,1)} %bitcast.11), channel_id=1, source_target_pairs={{0,4},{4,8},{8,12},{12,16},{16,20},{20,24},{24,28},{1,5},{5,9},{9,... | collective-permute-start | bytes 98312 | tf_op jit(solution)/shard_map/ppermute | solution.py:20
  131.7 3.5 %convolution_convert_fusion = bf16[2048,128]{1,0:T(8,128)(2,1)S(1)} fusion(bf16[2048,2880]{0,1:T(8,128)(2,1)S(1)} %copy-done.5, bf16[2880,128]{1,0:T(8,128)(2,1)S(1)} %copy-done.6), kind=kOutput, calls=%fused_computation.39 | convolution fusion | flops 1510211584 | bytes 13058048 | tf_op jit(solution)/shard_map/dot_general | solution.py:79
  135.3 3.1 %collective-permute-start.1 = (bf16[128,128]{1,0:T(8,128)(2,1)S(1)}, bf16[128,128]{1,0:T(8,128)(2,1)S(1)}, u32[]{:S(2)}, u32[]{:S(2)}) collective-permute-start(bf16[128,128]{1,0:T(8,128)(2,1)S(1)} %slice.73), channel_id=1, source_target_pairs={{0,4},{4,8},{8,12},{12,16},{16,20},{20,24},{24,28},{1,5},{5,9},{9,... | collective-permute-start | bytes 98312 | tf_op jit(solution)/shard_map/ppermute | solution.py:20
  138.4 7.2 %fusion.32 = f32[2048,512]{0,1:T(8,128)S(1)} fusion(bf16[2048,2880]{0,1:T(8,128)(2,1)S(1)} %copy-done.5, bf16[2880,512]{1,0:T(8,128)(2,1)S(1)} %copy-done), kind=kOutput, calls=%fused_computation.64 | convolution fusion | flops 6039797760 | bytes 18939904 | tf_op jit(solution)/shard_map/dot_general | solution.py:77
  145.6 0.7 subtract_convert_fusion
  146.5 1.1 copy.16
  147.6 42.9 %while.12 = (s32[]{:T(128)}, bf16[4,512,512]{1,2,0:T(8,128)(2,1)}, s32[4]{0:T(128)S(1)}, bf16[2176,2,64]{0,2,1:T(8,128)(2,1)}, s32[2176]{0:T(1024)S(1)}, /*index...) while((s32[]{:T(128)}, bf16[4,512,512]{1,2,0:T(8,128)(2,1)}, ...), condition=%wide.region_4.5_spmd, body=%wide.region_1.4_spmd.sunk | while | flops 702407808 | bytes 35308540 | solution.py:111
  147.9 0.6 dynamic_slice.78
  149.3 0.7 compare_and_fusion.2
  150.0 1.8 fusion.47
  151.8 2.2 fusion.48
  154.0 3.7 %divide_convert_fusion.2 = bf16[512,2,4,64]{0,3,2,1:T(8,128)(2,1)S(1)} fusion(f32[2,640,512,4]{2,1,3,0:T(8,128)S(1)} %get-tuple-element.248, f32[2,4,512]{2,1,0:T(4,128)S(1)} %get-tuple-element.249, pred[512,640]{0,1:T(8,128)(4,1)S(1)} %compare_and_fusion.2, f32[512,2,4]{0,2,1:T(4,128)S(1)} %bitcast.75, bf16[2176,2,64]{0,2,1:T(8,128)(2,1)} %get-tuple-element.283, ...), kind=kOutput, calls=%fused_computation.9.clone.1 | convolution fusion | flops 346554368 | bytes 11534340 | tf_op jit(solution)/shard_map/while/body/eval_jaxpr/hgqk,khd->qhgd/dot_general | solution.py:52
  157.7 0.8 constant_dynamic-update-slice_fusion.2
  160.0 0.7 compare_and_fusion.2
  160.7 1.8 fusion.47
  162.4 2.2 fusion.48
  164.6 3.7 %divide_convert_fusion.2 = bf16[512,2,4,64]{0,3,2,1:T(8,128)(2,1)S(1)} fusion(f32[2,640,512,4]{2,1,3,0:T(8,128)S(1)} %get-tuple-element.248, f32[2,4,512]{2,1,0:T(4,128)S(1)} %get-tuple-element.249, pred[512,640]{0,1:T(8,128)(4,1)S(1)} %compare_and_fusion.2, f32[512,2,4]{0,2,1:T(4,128)S(1)} %bitcast.75, bf16[2176,2,64]{0,2,1:T(8,128)(2,1)} %get-tuple-element.283, ...), kind=kOutput, calls=%fused_computation.9.clone.1 | convolution fusion | flops 346554368 | bytes 11534340 | tf_op jit(solution)/shard_map/while/body/eval_jaxpr/hgqk,khd->qhgd/dot_general | solution.py:52
  168.3 0.8 constant_dynamic-update-slice_fusion.2
  169.2 0.6 dynamic_slice.78
  170.6 0.7 compare_and_fusion.2
  171.3 1.8 fusion.47
  173.1 2.2 fusion.48
  175.2 3.7 %divide_convert_fusion.2 = bf16[512,2,4,64]{0,3,2,1:T(8,128)(2,1)S(1)} fusion(f32[2,640,512,4]{2,1,3,0:T(8,128)S(1)} %get-tuple-element.248, f32[2,4,512]{2,1,0:T(4,128)S(1)} %get-tuple-element.249, pred[512,640]{0,1:T(8,128)(4,1)S(1)} %compare_and_fusion.2, f32[512,2,4]{0,2,1:T(4,128)S(1)} %bitcast.75, bf16[2176,2,64]{0,2,1:T(8,128)(2,1)} %get-tuple-element.283, ...), kind=kOutput, calls=%fused_computation.9.clone.1 | convolution fusion | flops 346554368 | bytes 11534340 | tf_op jit(solution)/shard_map/while/body/eval_jaxpr/hgqk,khd->qhgd/dot_general | solution.py:52
  179.0 0.9 constant_dynamic-update-slice_fusion.2
  181.3 0.7 compare_and_fusion.2
  182.0 1.8 fusion.47
  183.8 2.2 fusion.48
  185.9 3.7 %divide_convert_fusion.2 = bf16[512,2,4,64]{0,3,2,1:T(8,128)(2,1)S(1)} fusion(f32[2,640,512,4]{2,1,3,0:T(8,128)S(1)} %get-tuple-element.248, f32[2,4,512]{2,1,0:T(4,128)S(1)} %get-tuple-element.249, pred[512,640]{0,1:T(8,128)(4,1)S(1)} %compare_and_fusion.2, f32[512,2,4]{0,2,1:T(4,128)S(1)} %bitcast.75, bf16[2176,2,64]{0,2,1:T(8,128)(2,1)} %get-tuple-element.283, ...), kind=kOutput, calls=%fused_computation.9.clone.1 | convolution fusion | flops 346554368 | bytes 11534340 | tf_op jit(solution)/shard_map/while/body/eval_jaxpr/hgqk,khd->qhgd/dot_general | solution.py:52
  189.7 0.9 constant_dynamic-update-slice_fusion.2
  190.5 5.2 %all-to-all-start = ((bf16[4,512,512]{1,2,0:T(8,128)(2,1)}), bf16[4,512,512]{1,2,0:T(8,128)(2,1)}, u32[]{:S(2)}, u32[]{:S(2)}) async-start(bf16[4,512,512]{1,2,0:T(8,128)(2,1)} %get-tuple-element.130), calls=%async_computation | async-start | bytes 4194304 | tf_op jit(solution)/shard_map/all_to_all | solution.py:113
  195.8 11.5 %all-gather.5.cloned.1.call-done = bf16[2048,2880]{0,1:T(8,128)(2,1)} async-done(((bf16[512,2880]{0,1:T(8,128)(2,1)}), bf16[2048,2880]{0,1:T(8,128)(2,1)}) %all-gather.5.cloned.1.call-update) | async-done | bytes 11796496 | tf_op jit(solution)/shard_map/all_gather | solution.py:116
  207.2 17.8 %all-to-all-done = bf16[4,512,512]{1,2,0:T(8,128)(2,1)} async-done(((bf16[4,512,512]{1,2,0:T(8,128)(2,1)}), bf16[4,512,512]{1,2,0:T(8,128)(2,1)}, u32[]{:S(2)}, u32[]{:S(2)}) %all-to-all-start) | async-done | bytes 2097184 | tf_op jit(solution)/shard_map/all_to_all | solution.py:113
  225.0 13.2 %fusion.24 = bf16[512,2880]{0,1:T(8,128)(2,1)} fusion(bf16[512,2880]{0,1:T(8,128)(2,1)} %param.10, bf16[2048,2880]{0,1:T(8,128)(2,1)} %all-gather.5.cloned.1.call-done, bf16[512,2048]{0,1:T(8,128)(2,1)} %bitcast.17), kind=kOutput, calls=%fused_computation.29 | convolution fusion | flops 6044221440 | bytes 19791872 | tf_op jit(solution)/shard_map/dot_general | solution.py:114
  (54 shorter events, 3.1 us)
Async XLA Ops:
  6.5 131.8 %copy-start = (bf16[2880,512]{1,0:T(8,128)(2,1)S(1)}, bf16[2880,512]{1,0:T(8,128)(2,1)}, u32[]{:S(2)}) copy-start(bf16[2880,512]{1,0:T(8,128)(2,1)} %param.13) | copy-start | bytes 8847364
  6.5 15.6 %copy-start.3 = (f32[4,2880]{1,0:T(4,128)S(1)}, f32[4,2880]{1,0:T(4,128)}, u32[]{:S(2)}) copy-start(f32[4,2880]{1,0:T(4,128)} %param.12) | copy-start | bytes 138244
  6.5 114.7 %all-gather.3.cloned.1.call-start = ((), (), s32[]{:S(2)}) async-start(), calls=%async_computation.1 | async-start | bytes 14745600 | tf_op jit(solution)/shard_map/all_gather | solution.py:74
  11.8 1.6 copy-start.2
  15.9 7.1 %collective-permute-start = (bf16[3,2880]{1,0:T(4,128)(2,1)S(1)}, bf16[3,2880]{1,0:T(4,128)(2,1)S(1)}, u32[]{:S(2)}, u32[]{:S(2)}) collective-permute-start(bf16[3,2880]{1,0:T(4,128)(2,1)S(1)} %copy.14), channel_id=1, source_target_pairs={{0,1},{1,2},{2,3},{3,4},{4,5},{5,6},{6,7},{7,8},{8,9},{9,10},{10,1... | collective-permute-start | bytes 51848 | tf_op jit(solution)/shard_map/ppermute | solution.py:20
  27.9 8.4 %copy-start.4 = (s32[2048]{0:T(1024)S(1)}, s32[2048]{0:T(1024)}, u32[]{:S(2)}) copy-start(s32[2048]{0:T(1024)} %param.17) | copy-start | bytes 24580
  36.2 171.0 %all-gather.5.cloned.1.call-start = ((), (), s32[]{:S(2)}) async-start(), calls=%async_computation.2 | async-start | bytes 14745600 | tf_op jit(solution)/shard_map/all_gather | solution.py:116
  36.3 4.2 %collective-permute-start.2 = (s32[128]{0:T(128)S(1)}, s32[128]{0:T(128)S(1)}, u32[]{:S(2)}, u32[]{:S(2)}) collective-permute-start(s32[128]{0:T(128)S(1)} %slice.61), channel_id=1, source_target_pairs={{0,4},{4,8},{8,12},{12,16},{16,20},{20,24},{24,28},{1,5},{5,9},{9,... | collective-permute-start | bytes 1544 | tf_op jit(solution)/shard_map/ppermute | solution.py:20
  121.2 10.5 %copy-start.5 = (bf16[2048,2880]{0,1:T(8,128)(2,1)S(1)}, bf16[2048,2880]{0,1:T(8,128)(2,1)}, u32[]{:S(2)}) copy-start(bf16[2048,2880]{0,1:T(8,128)(2,1)} %all-gather.3.cloned.1.call-done) | copy-start | bytes 35389444
  121.2 10.5 %copy-start.6 = (bf16[2880,128]{1,0:T(8,128)(2,1)S(1)}, bf16[2880,128]{1,0:T(8,128)(2,1)}, u32[]{:S(2)}) copy-start(bf16[2880,128]{1,0:T(8,128)(2,1)} %param.15) | copy-start | bytes 2211844
  128.4 19.1 %collective-permute-start.3 = (bf16[128,128]{0,1:T(8,128)(2,1)}, bf16[128,128]{0,1:T(8,128)(2,1)S(1)}, u32[]{:S(2)}, u32[]{:S(2)}) collective-permute-start(bf16[128,128]{0,1:T(8,128)(2,1)} %bitcast.11), channel_id=1, source_target_pairs={{0,4},{4,8},{8,12},{12,16},{16,20},{20,24},{24,28},{1,5},{5,9},{9,... | collective-permute-start | bytes 98312 | tf_op jit(solution)/shard_map/ppermute | solution.py:20
  135.3 11.2 %collective-permute-start.1 = (bf16[128,128]{1,0:T(8,128)(2,1)S(1)}, bf16[128,128]{1,0:T(8,128)(2,1)S(1)}, u32[]{:S(2)}, u32[]{:S(2)}) collective-permute-start(bf16[128,128]{1,0:T(8,128)(2,1)S(1)} %slice.73), channel_id=1, source_target_pairs={{0,4},{4,8},{8,12},{12,16},{16,20},{20,24},{24,28},{1,5},{5,9},{9,... | collective-permute-start | bytes 98312 | tf_op jit(solution)/shard_map/ppermute | solution.py:20
  190.5 34.5 %all-to-all-start = ((bf16[4,512,512]{1,2,0:T(8,128)(2,1)}), bf16[4,512,512]{1,2,0:T(8,128)(2,1)}, u32[]{:S(2)}, u32[]{:S(2)}) async-start(bf16[4,512,512]{1,2,0:T(8,128)(2,1)} %get-tuple-element.130), calls=%async_computation | async-start | bytes 4194304 | tf_op jit(solution)/shard_map/all_to_all | solution.py:113
  225.0 13.2 %copy-start.1 = (bf16[2880,512]{1,0:T(8,128)(2,1)S(1)}, bf16[2880,512]{1,0:T(8,128)(2,1)}, u32[]{:S(2)}) copy-start(bf16[2880,512]{1,0:T(8,128)(2,1)} %param.13) | copy-start | bytes 8847364
Sparse Core Ops, SparseCore 0:
  36.4 84.7 all-gather.2
  122.9 84.3 all-gather.4
where the time goes:
time: 245 us
  waiting for transfers between devices  111 us (45%)
  matrix products  52.4 us (21%)
  other arithmetic  31.9 us (13%)
  starting transfers between devices  20.9 us (9%)
  between operations  13.7 us (6%)
  local copies, waits for them, and re-layouts  12.9 us (5%)
  loops' own time  2.61 us (1%)
    all_gather x1, waiting for transfers between devices, local(): piece = lax.all_gather(mixed, 'tensor', axis=0, tiled=True)  80.6 us
    all_to_all x1, waiting for transfers between devices, local(): lax.all_to_all(attended, 'tensor', split_axis=0, concat_axis=1, tiled=True)  17.8 us
    ppermute x4, starting transfers between devices, passed_along(): return lax.ppermute(array, axis, pairs)  15.7 us
    dot_general x4, matrix products, attend(): jnp.einsum('hgqk,khd->qhgd', rounded, values, preferred_element_type=jnp....  14.9 us
    dot_general x1, matrix products, local(): jnp.dot(regrouped, lax.all_gather(w_out, 'tensor', axis=0, tiled=True), p...  13.2 us
    all_gather x1, waiting for transfers between devices, local(): lax.all_gather(w_out, 'tensor', axis=0, tiled=True)  11.5 us
    reduce_sum x4, other arithmetic, attend(): total = jnp.sum(weights, axis=3)  8.69 us
    convert_element_type x1, other arithmetic, local(): mixed = convolved.astype(jnp.bfloat16)  8.31 us
  transfers between devices with their start and end apart: 7, of which 4 were waited for; matrix products, arithmetic and copies ran while one was open for 25% of the time, Pallas kernels for 0%

commit v1 on v0

v1 whole, which is shorter than its diff:
```python
import math

import jax
import jax.numpy as jnp
import numpy as np
from jax import lax
from jax.experimental import pallas as pl
from jax.experimental.pallas import tpu as pltpu
from jax.sharding import PartitionSpec as P

HEAD = 64
WINDOW = 128
EPS = 1e-05
ROPE_BASE = 150000.0
NEG = -1e30
MESH = pl.DeviceIdType.MESH

D = 2880
ROWS = 512
CHIP = 2 * ROWS
NB = CHIP // WINDOW
HALO = 16
CB = 64
NCB = ROWS // CB
GM = 256
PIECE = D // 8
CHUNKS = 5
A, B, AL, AR, BL, BR, ALL_, BRR = range(8)


def rope_tables():
    half = HEAD // 2
    frequency = np.exp(np.arange(half) * (-2.0 * math.log(ROPE_BASE) / HEAD))
    lanes = np.tile(frequency, 4)
    inner = np.arange(WINDOW)[:, None] * lanes[None, :]
    outer = (np.arange(128) * WINDOW)[:, None] * lanes[None, :]
    return np.stack([np.cos(inner), np.sin(inner), np.cos(outer), np.sin(outer)]).astype(np.float32)


def kernel(
    hid_h, gain_h, conv_h, wq_h, wk_h, wv_h, wo_h, doc_h, rope_h, out_h,
    hid, gain, conv, mixed, w, wo, rope, cosv, sinv, doc, dprev, docx, bias,
    q, kx, vx, tail, halo, att, psend, precv, outv,
    load_sem, wsem_s, wsem_r, mix_s, mix_r, edge_s, edge_r, kv_s, kv_r, part_s, part_r, out_sem,
):
    dp, seq, tensor = lax.axis_index("dp"), lax.axis_index("seq"), lax.axis_index("tensor")
    yh, core = tensor // 2, tensor % 2
    yl, x = seq // 4, seq % 4
    cross = (dp, (1 - yl) * 4 + x, (1 - yh) * 2 + core)
    ylo = (dp, (1 - yl) * 4 + x, tensor)
    right = ((dp, yl * 4 + (x + 1) % 4, tensor), ((dp + 1) % 4, seq, tensor))
    left = ((dp, yl * 4 + (x + 3) % 4, tensor), ((dp + 3) % 4, seq, tensor))
    partner = (dp, seq, yh * 2 + (1 - core))
    place = seq * 2 + yh
    nplace, pplace = (place + 1) % 16, (place + 15) % 16
    next_chip = (dp, nplace // 2, (nplace % 2) * 2 + core)
    prev_chip = (dp, pplace // 2, (pplace % 2) * 2 + core)
    order = seq * 4 + tensor
    norder, porder = (order + 1) % 32, (order + 31) % 32
    next_dev = (dp, norder // 4, norder % 4)
    prev_dev = (dp, porder // 4, porder % 4)
    ring = (x, dp)

    own = pl.multiple_of(core * ROWS, ROWS)
    other = pl.multiple_of((1 - core) * ROWS, ROWS)

    def local(i, src, dst):
        return pltpu.make_async_copy(src, dst, load_sem.at[i])

    doc_rows = pl.ds(pl.multiple_of(yh * 8, 8), 8)
    loads = [
        local(0, hid_h, hid.at[pl.ds(HALO, ROWS)]),
        local(1, gain_h, gain),
        local(2, conv_h, conv),
        local(3, rope_h, rope),
        local(4, doc_h.at[doc_rows], doc),
        local(5, wk_h, w.at[0, 0]),
        local(6, wv_h, w.at[0, 3]),
        local(7, wq_h.at[:, pl.ds(0, 128)], w.at[0, 1]),
        local(8, wq_h.at[:, pl.ds(128, 128)], w.at[0, 2]),
        local(9, wq_h.at[:, pl.ds(256, 128)], w.at[0, 4]),
        local(10, wq_h.at[:, pl.ds(384, 128)], w.at[0, 5]),
        local(11, wo_h, wo.at[pl.ds(0, 512)]),
    ]
    for load in loads:
        load.start()

    barrier = pltpu.get_barrier_semaphore()
    peers = [cross, ylo, *right, *left, partner, next_chip, prev_chip, next_dev, prev_dev]
    for peer in peers:
        pl.semaphore_signal(barrier, inc=1, device_id=peer, device_id_type=MESH)
    pl.semaphore_wait(barrier, len(peers))

    def remote(src, dst, send, recv, device):
        return pltpu.make_async_remote_copy(
            src_ref=src, dst_ref=dst, send_sem=send, recv_sem=recv,
            device_id=device, device_id_type=MESH,
        )

    def piece(s, c, at, l):
        if c < 3:
            start = pl.multiple_of(at * (2 * PIECE) + l * PIECE, 8)
            return w.at[1, s * 3 + c, pl.ds(start, PIECE)]
        start = pl.multiple_of(512 + s * 256 + (c - 3) * 128 + (at * 2 + l) * 16, 16)
        return wo.at[pl.ds(start, 16)]

    def source(s, c, at, l):
        if c < 3:
            rows = pl.ds(pl.multiple_of(at * (2 * PIECE) + l * PIECE, 8), PIECE)
            if c == 0:
                return (wk_h, wv_h)[s].at[rows]
            return wq_h.at[rows, pl.ds(s * 256 + (c - 1) * 128, 128)]
        start = pl.multiple_of(s * 256 + (c - 3) * 128 + (at * 2 + l) * 16, 16)
        return wo_h.at[pl.ds(start, 16)]

    sent = []

    def send(s, c, kind, src, dst, device):
        copy = remote(src, dst, wsem_s.at[s, c, kind], wsem_r.at[s, c, kind], device)
        copy.start()
        sent.append(copy)

    def arrived(s, c, kind, at, l):
        ref = piece(s, c, at, l)
        remote(ref, ref, wsem_s.at[s, c, kind], wsem_r.at[s, c, kind], cross).wait_recv()

    def before(s):
        return (ring[s] + 3) % 4

    def after(s):
        return (ring[s] + 1) % 4

    def over(s):
        return (ring[s] + 2) % 4

    def s0(c):
        for s in range(2):
            arrived(s, c, A, ring[s], yl)
            ref = piece(s, c, ring[s], yl)
            send(s, c, AL, ref, ref, right[s])
            send(s, c, AR, ref, ref, left[s])
            send(s, c, B, ref, ref, ylo)

    def s1(c):
        for s in range(2):
            arrived(s, c, B, ring[s], 1 - yl)
            ref = piece(s, c, ring[s], 1 - yl)
            send(s, c, BR, ref, ref, left[s])
            send(s, c, BL, ref, ref, right[s])
            arrived(s, c, AL, before(s), yl)
            ref = piece(s, c, before(s), yl)
            send(s, c, ALL_, ref, ref, right[s])

    def s2(c):
        for s in range(2):
            arrived(s, c, BR, after(s), 1 - yl)
            ref = piece(s, c, after(s), 1 - yl)
            send(s, c, BRR, ref, ref, left[s])

    def s3(c):
        for s in range(2):
            arrived(s, c, AR, after(s), yl)
            arrived(s, c, BL, before(s), 1 - yl)
            arrived(s, c, ALL_, over(s), yl)
            arrived(s, c, BRR, over(s), 1 - yl)

    edge = [
        remote(hid_h.at[pl.ds(ROWS - HALO, HALO)], hid.at[pl.ds(0, HALO)], edge_s.at[0], edge_r.at[0], next_dev),
        remote(doc_h.at[doc_rows], dprev, edge_s.at[1], edge_r.at[1], next_chip),
    ]
    for copy in edge:
        copy.start()
    for c in range(CHUNKS):
        for s in range(2):
            send(s, c, A, source(s, c, ring[s], 1 - yl), piece(s, c, ring[s], 1 - yl), cross)

    for i in range(3):
        loads[i].wait()

    def norm_conv(b):
        base = pl.multiple_of(b * CB, CB)
        rows = pl.ds(base, CB + HALO)
        total = jnp.zeros((CB + 8, 128), jnp.float32)
        for lane in range(0, D - 64, 128):
            v = hid[rows, lane:lane + 128].astype(jnp.float32)[8:]
            total = total + v * v
        v = hid[rows, D - 64:D].astype(jnp.float32)[8:]
        square = jnp.sum(total, axis=1, keepdims=True) + jnp.sum(v * v, axis=1, keepdims=True)
        scale = lax.rsqrt(square * (1.0 / D) + EPS)
        first = jnp.logical_and(b == 0, order == 0)
        row = lax.broadcasted_iota(jnp.int32, (CB + 8, 1), 0)
        keep = jnp.where(first, 0.0, 1.0)
        scale = jnp.where(row < 8, scale * keep, scale)
        at = pl.multiple_of(own + base, CB)
        for lane in range(0, D, 128):
            width = min(128, D - lane)
            cols = slice(lane, lane + width)
            v = hid[rows, cols].astype(jnp.float32)[8:]
            n = (v * scale * gain[:, cols]).astype(jnp.bfloat16).astype(jnp.float32)
            m = conv[0:1, cols] * n[8:]
            for tap in range(1, 4):
                m = m + conv[tap:tap + 1, cols] * pltpu.roll(n, tap, 0)[8:]
            mixed[pl.ds(at, CB), cols] = m.astype(jnp.bfloat16)

    def mix_copy(b, start):
        rows = pl.ds(pl.multiple_of(start + b * CB, CB), CB)
        return remote(mixed.at[rows], mixed.at[rows], mix_s.at[b], mix_r.at[b], partner)

    def norm_step(b, carry):
        norm_conv(b)
        mix_copy(b, own).start()
        return carry

    lax.fori_loop(1, 4, norm_step, 0)
    s0(0)
    lax.fori_loop(4, 6, norm_step, 0)
    s0(1)
    lax.fori_loop(6, NCB, norm_step, 0)
    edge[0].wait()
    norm_step(0, 0)
    s1(0)
    s0(2)

    loads[3].wait()
    loads[4].wait()
    edge[1].wait()
    lane = lax.broadcasted_iota(jnp.int32, (1, 128), 1)
    sign = jnp.where(lane % 64 < 32, -1.0, 1.0)
    docx[0:1, :] = jnp.where(place == 0, -1.0, dprev[7:8, :].astype(jnp.float32))
    docx[1:9, :] = doc[...].astype(jnp.float32)

    def table_step(b, carry):
        rows = pl.ds(pl.multiple_of(b * WINDOW, WINDOW), WINDOW)
        cb = rope[2, pl.ds(place * NB + b, 1), :]
        sb = rope[3, pl.ds(place * NB + b, 1), :]
        cosv[rows, :] = rope[0] * cb - rope[1] * sb
        sinv[rows, :] = (rope[1] * cb + rope[0] * sb) * sign
        r = lax.broadcasted_iota(jnp.int32, (128, 128), 0)
        c = lax.broadcasted_iota(jnp.int32, (128, 128), 1)
        k0 = docx[pl.ds(b, 1), :]
        k1 = docx[pl.ds(b + 1, 1), :]
        mine = jnp.sum(jnp.where(r == c, k1, 0.0), axis=1, keepdims=True)
        bias[b, :, 0:128] = jnp.where(jnp.logical_and(c > r, k0 == mine), 0.0, NEG)
        bias[b, :, 128:256] = jnp.where(jnp.logical_and(c <= r, k1 == mine), 0.0, NEG)
        return carry

    lax.fori_loop(0, NB, table_step, 0)

    def spread(dst, g, rows, v):
        low = lax.broadcasted_iota(jnp.int32, v.shape, 1) < 64
        turned = pltpu.roll(v, 64, 1)
        dst[g, 0, rows, :] = jnp.where(low, v, 0.0).astype(jnp.bfloat16)
        dst[g, 1, rows, :] = jnp.where(low, 0.0, turned).astype(jnp.bfloat16)
        dst[g, 2, rows, :] = jnp.where(low, turned, 0.0).astype(jnp.bfloat16)
        dst[g, 3, rows, :] = jnp.where(low, 0.0, v).astype(jnp.bfloat16)

    def project(g, start):
        rows = pl.ds(start, GM)
        ext = pl.ds(pl.multiple_of(start + WINDOW, WINDOW), GM)
        weights = jnp.concatenate([w[g, j] for j in range(6)], axis=1)
        p = jnp.dot(mixed[rows, :], weights, preferred_element_type=jnp.float32)
        cosine, sine = cosv[rows, :], sinv[rows, :]
        low = lax.broadcasted_iota(jnp.int32, (GM, 128), 1) % 64 < 32

        def turn(v):
            return v * cosine + jnp.where(low, pltpu.roll(v, 96, 1), pltpu.roll(v, 32, 1)) * sine

        k = turn(p[:, 0:128])
        v = p[:, 384:512]
        spread(kx, g, ext, k)
        spread(vx, g, ext, v)
        tail[g, 0, rows, :] = k.astype(jnp.bfloat16)
        tail[g, 1, rows, :] = v.astype(jnp.bfloat16)
        for i, j in enumerate((1, 2, 4, 5)):
            v = turn(p[:, j * 128:(j + 1) * 128])
            q[g, rows, i * 128:(i + 1) * 128] = (v * 0.125).astype(jnp.bfloat16)

    def project_rows(g, start):
        def step(i, carry):
            project(g, pl.multiple_of(start + i * GM, GM))
            return carry

        lax.fori_loop(0, ROWS // GM, step, 0)

    def kv_copy(g, i):
        return remote(
            tail.at[g, i, pl.ds(CHIP - WINDOW, WINDOW)], halo.at[1 - g, i],
            kv_s.at[g, i], kv_r.at[1 - g, i], next_chip,
        )

    def attend(g, b):
        rows = pl.ds(pl.multiple_of(b * WINDOW, WINDOW), WINDOW)
        keys = pl.ds(pl.multiple_of(b * WINDOW, WINDOW), 2 * WINDOW)
        extra = bias[b]
        extra = jnp.concatenate([extra, extra], axis=0)
        low = lax.broadcasted_iota(jnp.int32, (256, 128), 1) < 64
        for j in range(2):
            cols = j * 256
            both = jnp.concatenate([q[g, rows, cols:cols + 128], q[g, rows, cols + 128:cols + 256]], axis=0)
            k2 = jnp.concatenate([kx[g, 2 * j, keys, :], kx[g, 2 * j + 1, keys, :]], axis=0)
            v2 = jnp.concatenate([vx[g, 2 * j, keys, :], vx[g, 2 * j + 1, keys, :]], axis=0)
            s = lax.dot_general(both, k2, (((1,), (1,)), ((), ())), preferred_element_type=jnp.float32)
            weights, inverse = [], []
            for i in range(2):
                half = s[:, i * 256:(i + 1) * 256] + extra
                e = jnp.exp(half - jnp.max(half, axis=1, keepdims=True))
                inverse.append(1.0 / jnp.sum(e, axis=1, keepdims=True))
                weights.append(e.astype(jnp.bfloat16))
            o = jnp.dot(jnp.concatenate(weights, axis=1), v2, preferred_element_type=jnp.float32)
            o = (o * jnp.where(low, inverse[0], inverse[1])).astype(jnp.bfloat16)
            att[rows, g * 512 + cols:g * 512 + cols + 128] = o[0:128]
            att[rows, g * 512 + cols + 128:g * 512 + cols + 256] = o[128:256]

    def attend_blocks(g, low, high):
        def step(b, carry):
            attend(g, b)
            return carry

        lax.fori_loop(low, high, step, 0)

    def attend_first(g):
        for i in range(2):
            copy = remote(
                halo.at[g, i], halo.at[g, i], kv_s.at[1 - g, i], kv_r.at[g, i], prev_chip
            )
            copy.wait_recv()
        spread(kx, g, pl.ds(0, WINDOW), halo[g, 0].astype(jnp.float32))
        spread(vx, g, pl.ds(0, WINDOW), halo[g, 1].astype(jnp.float32))
        attend(g, 0)

    for i in range(5, 11):
        loads[i].wait()
    project_rows(0, own)
    s1(1)
    s0(3)
    for b in range(NCB):
        mix_copy(b, other).wait_recv()
    project_rows(0, other)
    for i in range(2):
        kv_copy(0, i).start()
    s2(0)
    s1(2)
    s0(4)
    attend_blocks(0, 1, 4)
    s2(1)
    s1(3)
    attend_blocks(0, 4, 6)
    s2(2)
    attend_blocks(0, 6, 8)
    s1(4)
    for c in range(3):
        s3(c)
    project_rows(1, own)
    s2(3)
    project_rows(1, other)
    for i in range(2):
        kv_copy(1, i).start()
    s2(4)
    attend_first(0)
    attend_blocks(1, 1, 8)
    attend_first(1)

    loads[11].wait()
    for c in range(3, 5):
        s3(c)
    OM = 128

    def part_copy(i):
        rows = pl.ds(pl.multiple_of(i * OM, OM), OM)
        return remote(psend.at[rows], precv.at[rows], part_s.at[i], part_r.at[i], partner)

    def out_copy(i):
        rows = pl.ds(pl.multiple_of(i * OM, OM), OM)
        return pltpu.make_async_copy(outv.at[rows], out_h.at[rows], out_sem.at[i])

    def far_step(i, carry):
        p = jnp.dot(
            att[pl.ds(pl.multiple_of(other + i * OM, OM), OM), :], wo[...],
            preferred_element_type=jnp.float32,
        )
        psend[pl.ds(pl.multiple_of(i * OM, OM), OM), :] = p.astype(jnp.bfloat16)
        part_copy(i).start()
        return carry

    def near_step(i, carry):
        rows = pl.ds(pl.multiple_of(i * OM, OM), OM)
        p = jnp.dot(
            att[pl.ds(pl.multiple_of(own + i * OM, OM), OM), :], wo[...],
            preferred_element_type=jnp.float32,
        )
        part_copy(i).wait_recv()
        p = p + precv[rows, :].astype(jnp.float32)
        base = hid[pl.ds(pl.multiple_of(HALO + i * OM, 16), OM), :].astype(jnp.float32)
        outv[rows, :] = (base + p).astype(jnp.bfloat16)
        out_copy(i).start()
        return carry

    lax.fori_loop(0, ROWS // OM, far_step, 0)
    lax.fori_loop(0, ROWS // OM, near_step, 0)

    for i in range(ROWS // OM):
        out_copy(i).wait()
        part_copy(i).wait_send()
    for b in range(NCB):
        mix_copy(b, own).wait_send()
    for g in range(2):
        for i in range(2):
            kv_copy(g, i).wait_send()
    for copy in sent:
        copy.wait_send()


def local(hidden_in, norm_gain, conv_weight, w_query, w_key, w_value, w_out, doc_ids):
    bf16, f32 = jnp.bfloat16, jnp.float32
    vmem, dma = pltpu.VMEM, pltpu.SemaphoreType.DMA
    scratch = [
        vmem((HALO + ROWS, D), bf16),
        vmem((1, D), f32),
        vmem((4, D), f32),
        vmem((CHIP, D), bf16),
        vmem((2, 6, D, 128), bf16),
        vmem((1024, D), bf16),
        vmem((4, 128, 128), f32),
        vmem((CHIP, 128), f32),
        vmem((CHIP, 128), f32),
        vmem((8, 128), jnp.int32),
        vmem((8, 128), jnp.int32),
        vmem((16, 128), f32),
        vmem((NB, 128, 256), f32),
        vmem((2, CHIP, 512), bf16),
        vmem((2, 4, CHIP + WINDOW, 128), bf16),
        vmem((2, 4, CHIP + WINDOW, 128), bf16),
        vmem((2, 2, CHIP, 128), bf16),
        vmem((2, 2, WINDOW, 128), bf16),
        vmem((CHIP, 1024), bf16),
        vmem((ROWS, D), bf16),
        vmem((ROWS, D), bf16),
        vmem((ROWS, D), bf16),
        dma((12,)),
        dma((2, CHUNKS, 8)),
        dma((2, CHUNKS, 8)),
        dma((NCB,)),
        dma((NCB,)),
        dma((2,)),
        dma((2,)),
        dma((2, 2)),
        dma((2, 2)),
        dma((4,)),
        dma((4,)),
        dma((4,)),
    ]
    hbm = pl.BlockSpec(memory_space=pl.ANY)
    return pl.pallas_call(
        kernel,
        out_shape=jax.ShapeDtypeStruct((ROWS, D), bf16),
        in_specs=[hbm] * 9,
        out_specs=hbm,
        scratch_shapes=scratch,
        compiler_params=pltpu.CompilerParams(
            collective_id=0, has_side_effects=True, vmem_limit_bytes=67043328
        ),
        name="attention_block",
    )(
        hidden_in, norm_gain.reshape(1, D), conv_weight, w_query, w_key, w_value, w_out,
        doc_ids.reshape(16, 128), jnp.asarray(rope_tables()),
    )


def solution(mesh):
    in_specs = (
        P(("dp", "seq", "tensor"), None),
        P(),
        P(),
        P(None, "tensor"),
        P(None, "tensor"),
        P(None, "tensor"),
        P("tensor", None),
        P(("dp", "seq")),
    )
    out_specs = P(("dp", "seq", "tensor"), None)
    return jax.shard_map(local, mesh=mesh, in_specs=in_specs, out_specs=out_specs, check_vma=False)
```

time: 245 us -> 89.5 us (0.37)
  waiting for transfers between devices: 111 us -> 0 us
  Pallas kernels: 0 us -> 75.3 us
  matrix products: 52.4 us -> 0 us
  other arithmetic: 31.9 us -> 0 us
  starting transfers between devices: 20.9 us -> 0 us
  between operations: 13.7 us -> 0.01 us
  loops' own time: 2.61 us -> 0 us
    all_gather x2 -> x0, waiting for transfers between devices: 92.1 us -> none  [the longest x1 80.6 us: local(): piece = lax.all_gather(mixed, 'tensor', axis=0, tiled=True)]
    pallas_call x0 -> x1, Pallas kernels: none -> 75.3 us  [local(): pl.pallas_call(kernel, out_shape=jax.ShapeDtypeStruct((ROWS, D), bf16), i...]
    dot_general x12 -> x0, matrix products: 52.4 us -> none  [the longest x4 14.9 us: attend(): jnp.einsum('hgqk,khd->qhgd', rounded, values, preferred_element_type=jnp....]
    all_to_all x1 -> x0, waiting for transfers between devices: 17.8 us -> none  [local(): lax.all_to_all(attended, 'tensor', split_axis=0, concat_axis=1, tiled=True)]
    ppermute x4 -> x0, starting transfers between devices: 15.7 us -> none  [passed_along(): return lax.ppermute(array, axis, pairs)]
    convert_element_type x4 -> x0, other arithmetic: 14.5 us -> none  [the longest x1 8.31 us: local(): mixed = convolved.astype(jnp.bfloat16)]
    reduce_sum x5 -> x0, other arithmetic: 11.4 us -> none  [the longest x4 8.69 us: attend(): total = jnp.sum(weights, axis=3)]
    unnamed x14 -> x4, local copies, waits for them, and re-layouts: 1.62 us -> 7.73 us
  transfers between devices with their start and end apart: 7 -> 0, of which waited for: 4 -> 0; matrix products, arithmetic and copies ran while one was open for 25% -> 0% of each run, Pallas kernels for 0% -> 0%
where the time goes in v1:
time: 89.5 us; the launch traced here: 88.9 us
  Pallas kernels  75.3 us (84%)
  local copies, waits for them, and re-layouts  13.6 us (15%)
    pallas_call x1, Pallas kernels, local(): pl.pallas_call(kernel, out_shape=jax.ShapeDtypeStruct((ROWS, D), bf16), i...  75.3 us
    unnamed x4, local copies, waits for them, and re-layouts  7.73 us
    pallas_call x1, local copies, waits for them, and re-layouts, local(): pl.pallas_call(kernel, out_shape=jax.ShapeDtypeStruct((ROWS, D), bf16), i...  4.57 us

profile of v1, /device:TPU:1, one launch (start us, length us, event | category | flops | bytes accessed | tf_op | source)
XLA Modules:
  0.0 88.9 jit_solution(6574689172565919145)
XLA Ops:
  0.0 1.3 %reshape.6.gain_h = f32[1,2880]{1,0:T(1,128)} reshape(f32[2880]{0:T(1024)} %param.10) | data formatting | bytes 23040 | tf_op jit(solution)/shard_map/reshape | solution.py:464
  1.3 0.0 copy-start
  1.3 4.7 %copy.10.hid_h = bf16[512,2880]{1,0:T(8,128)(2,1)} copy(bf16[512,2880]{0,1:T(8,128)(2,1)} %param.9) | data formatting | bytes 5898240 | tf_op args[0]
  6.0 0.0 copy-done
  6.0 3.0 %copy.11.wo_h = bf16[512,2880]{1,0:T(8,128)(2,1)} copy(bf16[512,2880]{0,1:T(8,128)(2,1)S(1)} %copy-done) | data formatting | bytes 5898240 | tf_op args[6]
  9.0 75.3 %attention_block.1 = bf16[512,2880]{1,0:T(8,128)(2,1)} custom-call(bf16[512,2880]{1,0:T(8,128)(2,1)} %copy.10.hid_h, f32[1,2880]{1,0:T(1,128)} %reshape.6.gain_h, f32[4,2880]{1,0:T(4,128)} %conv_h.1, bf16[2880,512]{1,0:T(8,128)(2,1)} %wq_h.1, bf16[2880,128]{1,0:T(8,128)(2,1)} %wk_h.1, bf16[2880,128]{1,0:T(8,128)(2,1)} %wv_h.1, bf16[512,2880]{1,0:T(8,128)(2,1)} %copy.11.wo_h, ...), custom_call_target="tpu_custom_call" | custom-call | tf_op jit(solution)/shard_map/attention_block/pallas_call | solution.py:453
  84.4 4.6 %copy.12 = bf16[512,2880]{0,1:T(8,128)(2,1)} copy(bf16[512,2880]{1,0:T(8,128)(2,1)} %attention_block.1) | data formatting | bytes 5898240 | tf_op jit(solution)/shard_map/attention_block/pallas_call | solution.py:453
Async XLA Ops:
  1.3 4.7 %copy-start = (bf16[512,2880]{0,1:T(8,128)(2,1)S(1)}, bf16[512,2880]{0,1:T(8,128)(2,1)}, u32[]{:S(2)}) copy-start(bf16[512,2880]{0,1:T(8,128)(2,1)} %param.15) | copy-start | bytes 8847364

commit v2 on v1

v2 whole, which is shorter than its diff:
```python
import math

import jax
import jax.numpy as jnp
import numpy as np
from jax import lax
from jax.experimental import pallas as pl
from jax.experimental.pallas import tpu as pltpu
from jax.sharding import PartitionSpec as P

HEAD = 64
WINDOW = 128
EPS = 1e-05
ROPE_BASE = 150000.0
NEG = -1e30
MESH = pl.DeviceIdType.MESH

D = 2880
ROWS = 512
CHIP = 2 * ROWS
NB = CHIP // WINDOW
HALO = 16
TB = 256
FC = D // 4
CB = 64
NCB = ROWS // CB
PIECE = D // 8
CHUNKS = 5
SLOTS = (
    ((0, 0),),
    ((0, 1), (1, 0)),
    ((0, 2),),
    ((2, 0), (1, 1)),
    ((0, 3),),
    ((2, 1), (1, 2)),
    ((0, 4),),
    ((2, 2), (1, 3)),
    (),
    ((2, 3),),
    ((1, 4),),
    ((2, 4),),
    (),
    (),
    (),
)
A, B, AL, AR, BL, BR, ALL_, BRR = range(8)


def rope_tables():
    half = HEAD // 2
    frequency = np.exp(np.arange(half) * (-2.0 * math.log(ROPE_BASE) / HEAD))
    lanes = np.tile(frequency, 4)
    inner = np.arange(WINDOW)[:, None] * lanes[None, :]
    outer = (np.arange(128) * WINDOW)[:, None] * lanes[None, :]
    return np.stack([np.cos(inner), np.sin(inner), np.cos(outer), np.sin(outer)]).astype(np.float32)


def kernel(
    hid_h, gain, conv_h, wq_h, wk_h, wv_h, wo_h, doc_h, rope_h, out_h,
    hid, flat, conv, mixed, w, rope, cosv, sinv, doc, dprev, docx, bias,
    q, kx, vx, tail, halo, att, acc, psend, precv,
    load_sem, wsem_s, wsem_r, mix_s, mix_r, edge_s, edge_r, kv_s, kv_r, part_s, part_r, out_sem,
):
    dp, seq, tensor = lax.axis_index("dp"), lax.axis_index("seq"), lax.axis_index("tensor")
    yh, core = tensor // 2, tensor % 2
    yl, x = seq // 4, seq % 4
    cross = (dp, (1 - yl) * 4 + x, (1 - yh) * 2 + core)
    ylo = (dp, (1 - yl) * 4 + x, tensor)
    right = ((dp, yl * 4 + (x + 1) % 4, tensor), ((dp + 1) % 4, seq, tensor))
    left = ((dp, yl * 4 + (x + 3) % 4, tensor), ((dp + 3) % 4, seq, tensor))
    partner = (dp, seq, yh * 2 + (1 - core))
    place = seq * 2 + yh
    nplace, pplace = (place + 1) % 16, (place + 15) % 16
    next_chip = (dp, nplace // 2, (nplace % 2) * 2 + core)
    prev_chip = (dp, pplace // 2, (pplace % 2) * 2 + core)
    order = seq * 4 + tensor
    norder, porder = (order + 1) % 32, (order + 31) % 32
    next_dev = (dp, norder // 4, norder % 4)
    prev_dev = (dp, porder // 4, porder % 4)
    ring = (x, dp)

    own = pl.multiple_of(core * ROWS, ROWS)
    other = pl.multiple_of((1 - core) * ROWS, ROWS)

    def local(i, src, dst):
        return pltpu.make_async_copy(src, dst, load_sem.at[i])

    doc_rows = pl.ds(pl.multiple_of(yh * 8, 8), 8)
    loads = [
        local(0, hid_h, flat),
        local(1, conv_h, conv),
        local(2, rope_h, rope),
        local(3, doc_h.at[doc_rows], doc),
        local(4, wk_h, w.at[0, 0]),
        local(5, wv_h, w.at[0, 5]),
    ]
    for j in range(4):
        cols = pl.ds(j * 128, 128)
        loads.append(local(6 + j, wq_h.at[:, cols], w.at[0, (j % 2) * 5 + 1 + j // 2]))
    for j in range(4):
        cols = pl.ds(j * 128, 128)
        loads.append(local(10 + j, wo_h.at[:, cols], w.at[0, (j % 2) * 5 + 3 + j // 2]))
    for load in loads:
        load.start()

    barrier = pltpu.get_barrier_semaphore()
    peers = [cross, ylo, *right, *left, partner, next_chip, prev_chip, next_dev, prev_dev]
    for peer in peers:
        pl.semaphore_signal(barrier, inc=1, device_id=peer, device_id_type=MESH)
    pl.semaphore_wait(barrier, len(peers))

    def remote(src, dst, send, recv, device):
        return pltpu.make_async_remote_copy(
            src_ref=src, dst_ref=dst, send_sem=send, recv_sem=recv,
            device_id=device, device_id_type=MESH,
        )

    def span(at, l):
        return pl.ds(pl.multiple_of(at * (2 * PIECE) + l * PIECE, 8), PIECE)

    def piece(s, c, at, l):
        return w.at[1, s * CHUNKS + c, span(at, l)]

    def source(s, c, at, l):
        if c == 0:
            return (wk_h, wv_h)[s].at[span(at, l)]
        ref = wq_h if c < 3 else wo_h
        return ref.at[span(at, l), pl.ds((((c - 1) % 2) * 2 + s) * 128, 128)]

    sent = []

    def send(s, c, kind, src, dst, device):
        copy = remote(src, dst, wsem_s.at[s, c, kind], wsem_r.at[s, c, kind], device)
        copy.start()
        sent.append(copy)

    def arrived(s, c, kind, at, l):
        ref = piece(s, c, at, l)
        remote(ref, ref, wsem_s.at[s, c, kind], wsem_r.at[s, c, kind], cross).wait_recv()

    def before(s):
        return (ring[s] + 3) % 4

    def after(s):
        return (ring[s] + 1) % 4

    def over(s):
        return (ring[s] + 2) % 4

    def s0(c):
        for s in range(2):
            arrived(s, c, A, ring[s], yl)
            ref = piece(s, c, ring[s], yl)
            send(s, c, AL, ref, ref, right[s])
            send(s, c, AR, ref, ref, left[s])
            send(s, c, B, ref, ref, ylo)

    def s1(c):
        for s in range(2):
            arrived(s, c, B, ring[s], 1 - yl)
            ref = piece(s, c, ring[s], 1 - yl)
            send(s, c, BR, ref, ref, left[s])
            send(s, c, BL, ref, ref, right[s])
            arrived(s, c, AL, before(s), yl)
            ref = piece(s, c, before(s), yl)
            send(s, c, ALL_, ref, ref, right[s])

    def s2(c):
        for s in range(2):
            arrived(s, c, BR, after(s), 1 - yl)
            ref = piece(s, c, after(s), 1 - yl)
            send(s, c, BRR, ref, ref, left[s])

    def s3(c):
        for s in range(2):
            arrived(s, c, AR, after(s), yl)
            arrived(s, c, BL, before(s), 1 - yl)
            arrived(s, c, ALL_, over(s), yl)
            arrived(s, c, BRR, over(s), 1 - yl)

    stages = (s0, s1, s2)

    def slot(i):
        for stage, c in SLOTS[i]:
            stages[stage](c)

    edge = [
        remote(hid.at[pl.ds(HALO + ROWS - 8, 8)], hid.at[pl.ds(8, 8)], edge_s.at[0], edge_r.at[0], next_dev),
        remote(doc_h.at[doc_rows], dprev, edge_s.at[1], edge_r.at[1], next_chip),
    ]
    for c in range(CHUNKS):
        for s in range(2):
            send(s, c, A, source(s, c, ring[s], 1 - yl), piece(s, c, ring[s], 1 - yl), cross)
    edge[1].start()

    for i in range(2):
        loads[i].wait()
    unit = lax.broadcasted_iota(jnp.int32, (TB, TB), 0) == lax.broadcasted_iota(jnp.int32, (TB, TB), 1)
    unit = jnp.where(unit, 1.0, 0.0).astype(jnp.bfloat16)

    def transpose(i):
        for f in range(0, D, 768):
            rows = slice(f, min(f + 768, D))
            turned = lax.dot_general(
                unit, flat[rows, i * TB:(i + 1) * TB], (((1,), (1,)), ((), ())),
                preferred_element_type=jnp.float32,
            )
            hid[HALO + i * TB:HALO + (i + 1) * TB, rows] = turned.astype(jnp.bfloat16)

    transpose(1)
    transpose(0)
    edge[0].start()

    def norm_conv(b):
        base = pl.multiple_of(b * CB, CB)
        rows = pl.ds(base, CB + HALO)
        total = jnp.zeros((CB + 8, 128), jnp.float32)
        for lane in range(0, D - 64, 128):
            v = hid[rows, lane:lane + 128].astype(jnp.float32)[8:]
            total = total + v * v
        v = hid[rows, D - 64:D].astype(jnp.float32)[8:]
        square = jnp.sum(total, axis=1, keepdims=True) + jnp.sum(v * v, axis=1, keepdims=True)
        scale = lax.rsqrt(square * (1.0 / D) + EPS)
        first = jnp.logical_and(b == 0, order == 0)
        row = lax.broadcasted_iota(jnp.int32, (CB + 8, 1), 0)
        keep = jnp.where(first, 0.0, 1.0)
        scale = jnp.where(row < 8, scale * keep, scale)
        at = pl.multiple_of(own + base, CB)
        for lane in range(0, D, 128):
            width = min(128, D - lane)
            cols = slice(lane, lane + width)
            v = hid[rows, cols].astype(jnp.float32)[8:]
            n = (v * scale * gain[cols].reshape(1, width)).astype(jnp.bfloat16).astype(jnp.float32)
            m = conv[0:1, cols] * n[8:]
            for tap in range(1, 4):
                m = m + conv[tap:tap + 1, cols] * pltpu.roll(n, tap, 0)[8:]
            mixed[pl.ds(at, CB), cols] = m.astype(jnp.bfloat16)

    def mix_copy(b, start):
        rows = pl.ds(pl.multiple_of(start + b * CB, CB), CB)
        return remote(mixed.at[rows], mixed.at[rows], mix_s.at[b], mix_r.at[b], partner)

    def norm_step(b, carry):
        norm_conv(b)
        mix_copy(b, own).start()
        return carry

    lax.fori_loop(1, NCB, norm_step, 0)
    edge[0].wait()
    norm_step(0, 0)
    slot(0)

    loads[2].wait()
    loads[3].wait()
    edge[1].wait()
    lane = lax.broadcasted_iota(jnp.int32, (1, 128), 1)
    sign = jnp.where(lane % 64 < 32, -1.0, 1.0)
    docx[0:1, :] = jnp.where(place == 0, -1.0, dprev[7:8, :].astype(jnp.float32))
    docx[1:9, :] = doc[...].astype(jnp.float32)

    def table_step(b, carry):
        rows = pl.ds(pl.multiple_of(b * WINDOW, WINDOW), WINDOW)
        cb = rope[2, pl.ds(place * NB + b, 1), :]
        sb = rope[3, pl.ds(place * NB + b, 1), :]
        cosv[rows, :] = rope[0] * cb - rope[1] * sb
        sinv[rows, :] = (rope[1] * cb + rope[0] * sb) * sign
        r = lax.broadcasted_iota(jnp.int32, (128, 128), 0)
        c = lax.broadcasted_iota(jnp.int32, (128, 128), 1)
        k0 = docx[pl.ds(b, 1), :]
        k1 = docx[pl.ds(b + 1, 1), :]
        mine = jnp.sum(jnp.where(r == c, k1, 0.0), axis=1, keepdims=True)
        bias[b, :, 0:128] = jnp.where(jnp.logical_and(c > r, k0 == mine), 0.0, NEG)
        bias[b, :, 128:256] = jnp.where(jnp.logical_and(c <= r, k1 == mine), 0.0, NEG)
        return carry

    lax.fori_loop(0, NB, table_step, 0)

    def spread(dst, g, rows, v):
        low = lax.broadcasted_iota(jnp.int32, v.shape, 1) < 64
        turned = pltpu.roll(v, 64, 1)
        dst[g, 0, rows, :] = jnp.where(low, v, 0.0).astype(jnp.bfloat16)
        dst[g, 1, rows, :] = jnp.where(low, 0.0, turned).astype(jnp.bfloat16)
        dst[g, 2, rows, :] = jnp.where(low, turned, 0.0).astype(jnp.bfloat16)
        dst[g, 3, rows, :] = jnp.where(low, 0.0, v).astype(jnp.bfloat16)

    def product(g, rows, a, b):
        weights = jnp.concatenate([w[g, a], w[g, b]], axis=1)
        return jnp.dot(mixed[rows, :], weights, preferred_element_type=jnp.float32)

    def turn(v, rows):
        low = lax.broadcasted_iota(jnp.int32, (ROWS, 128), 1) % 64 < 32
        swapped = jnp.where(low, pltpu.roll(v, 96, 1), pltpu.roll(v, 32, 1))
        return v * cosv[rows, :] + swapped * sinv[rows, :]

    def project_kv(g, start):
        rows = pl.ds(start, ROWS)
        ext = pl.ds(pl.multiple_of(start + WINDOW, WINDOW), ROWS)
        p = product(g, rows, 0, CHUNKS)
        k = turn(p[:, 0:128], rows)
        v = p[:, 128:256]
        spread(kx, g, ext, k)
        spread(vx, g, ext, v)
        tail[g, 0, :, :] = k[ROWS - WINDOW:].astype(jnp.bfloat16)
        tail[g, 1, :, :] = v[ROWS - WINDOW:].astype(jnp.bfloat16)

    def project_q(g, j, start):
        rows = pl.ds(start, ROWS)
        p = product(g, rows, 1 + j, CHUNKS + 1 + j)
        for i in range(2):
            v = turn(p[:, i * 128:(i + 1) * 128], rows) * 0.125
            q[g, j, i, rows, :] = v.astype(jnp.bfloat16)

    def kv_range(g):
        def step(i, carry):
            project_kv(g, pl.multiple_of(i * ROWS, ROWS))
            return carry

        lax.fori_loop(0, 2, step, 0)
        for i in range(2):
            kv_copy(g, i).start()

    def q_range(g, low, high):
        def step(i, carry):
            project_q(g, i // 2, pl.multiple_of((i % 2) * ROWS, ROWS))
            return carry

        lax.fori_loop(low, high, step, 0)

    def kv_copy(g, i):
        return remote(
            tail.at[g, i], halo.at[1 - g, i],
            kv_s.at[g, i], kv_r.at[1 - g, i], next_chip,
        )

    def attend(g, j, b):
        rows = pl.ds(pl.multiple_of(b * WINDOW, WINDOW), WINDOW)
        keys = pl.ds(pl.multiple_of(b * WINDOW, WINDOW), 2 * WINDOW)
        extra = bias[b]
        extra = jnp.concatenate([extra, extra], axis=0)
        low = lax.broadcasted_iota(jnp.int32, (256, 128), 1) < 64
        both = jnp.concatenate([q[g, j, 0, rows, :], q[g, j, 1, rows, :]], axis=0)
        k2 = jnp.concatenate([kx[g, 2 * j, keys, :], kx[g, 2 * j + 1, keys, :]], axis=0)
        v2 = jnp.concatenate([vx[g, 2 * j, keys, :], vx[g, 2 * j + 1, keys, :]], axis=0)
        s = lax.dot_general(both, k2, (((1,), (1,)), ((), ())), preferred_element_type=jnp.float32)
        weights, inverse = [], []
        for i in range(2):
            half = s[:, i * 256:(i + 1) * 256] + extra
            e = jnp.exp(half - jnp.max(half, axis=1, keepdims=True))
            inverse.append(1.0 / jnp.sum(e, axis=1, keepdims=True))
            weights.append(e.astype(jnp.bfloat16))
        o = jnp.dot(jnp.concatenate(weights, axis=1), v2, preferred_element_type=jnp.float32)
        o = (o * jnp.where(low, inverse[0], inverse[1])).astype(jnp.bfloat16)
        att[g, rows, j * 256:j * 256 + 128] = o[0:128]
        att[g, rows, j * 256 + 128:j * 256 + 256] = o[128:256]

    def attend_blocks(g, heads, low, high):
        def step(b, carry):
            for j in heads:
                attend(g, j, b)
            return carry

        lax.fori_loop(low, high, step, 0)

    def halo_in(g):
        for i in range(2):
            copy = remote(
                halo.at[g, i], halo.at[g, i], kv_s.at[1 - g, i], kv_r.at[g, i], prev_chip
            )
            copy.wait_recv()
        spread(kx, g, pl.ds(0, WINDOW), halo[g, 0].astype(jnp.float32))
        spread(vx, g, pl.ds(0, WINDOW), halo[g, 1].astype(jnp.float32))

    def out_product(g, blocks, features, start):
        weights = jnp.concatenate([w[g, b, features, :] for b, _ in blocks], axis=1)
        low, high = blocks[0][1] * 128, blocks[-1][1] * 128 + 128
        return lax.dot_general(
            weights, att[g, pl.ds(start, ROWS), low:high], (((1,), (1,)), ((), ())),
            preferred_element_type=jnp.float32,
        )

    def feature_rows(i):
        return pl.ds(pl.multiple_of(i * FC, 8), FC)

    both_parts = ((3, 0), (CHUNKS + 3, 1), (4, 2), (CHUNKS + 4, 3))

    def out_own(h):
        def step(i, carry):
            acc[h, feature_rows(i), :] = out_product(0, both_parts, feature_rows(i), h * ROWS)
            return carry

        lax.fori_loop(0, 4, step, 0)

    def out_add():
        def step(i, carry):
            for h in range(2):
                acc[h, feature_rows(i), :] += out_product(1, both_parts[:2], feature_rows(i), h * ROWS)
            return carry

        lax.fori_loop(0, 4, step, 0)

    def part_copy(i):
        rows = feature_rows(i)
        return remote(psend.at[rows], precv.at[rows], part_s.at[i], part_r.at[i], partner)

    def out_copy(i):
        rows = feature_rows(i)
        return pltpu.make_async_copy(flat.at[rows], out_h.at[rows], out_sem.at[i])

    def far_step(i, carry):
        rows = feature_rows(i)
        p = acc[1 - core, rows, :] + out_product(1, both_parts[2:], rows, other)
        psend[rows, :] = p.astype(jnp.bfloat16)
        part_copy(i).start()
        return carry

    def near_step(i, carry):
        rows = feature_rows(i)
        p = acc[core, rows, :] + out_product(1, both_parts[2:], rows, own)
        part_copy(i).wait_recv()
        p = p + precv[rows, :].astype(jnp.float32)
        flat[rows, :] = (flat[rows, :].astype(jnp.float32) + p).astype(jnp.bfloat16)
        out_copy(i).start()
        return carry

    for i in range(4, 10):
        loads[i].wait()
    for b in range(NCB):
        mix_copy(b, other).wait_recv()
    kv_range(0)
    slot(1)
    q_range(0, 0, 2)
    slot(2)
    q_range(0, 2, 4)
    slot(3)
    attend_blocks(0, (0, 1), 1, 3)
    slot(4)
    attend_blocks(0, (0, 1), 3, 6)
    slot(5)
    attend_blocks(0, (0, 1), 6, 8)
    slot(6)
    for i in range(10, 14):
        loads[i].wait()
    out_own(1)
    slot(7)
    s3(0)
    kv_range(1)
    slot(8)
    s3(1)
    q_range(1, 0, 2)
    slot(9)
    halo_in(1)
    attend_blocks(1, (0,), 0, NB)
    slot(10)
    halo_in(0)
    attend_blocks(0, (0, 1), 0, 1)
    out_own(0)
    slot(11)
    s3(2)
    q_range(1, 2, 4)
    slot(12)
    attend_blocks(1, (1,), 0, NB)
    slot(13)
    s3(3)
    out_add()
    slot(14)
    s3(4)
    lax.fori_loop(0, 4, far_step, 0)
    lax.fori_loop(0, 4, near_step, 0)

    for i in range(4):
        out_copy(i).wait()
        part_copy(i).wait_send()
    for b in range(NCB):
        mix_copy(b, own).wait_send()
    for g in range(2):
        for i in range(2):
            kv_copy(g, i).wait_send()
    for copy in sent:
        copy.wait_send()


def local(hidden_in, norm_gain, conv_weight, w_query, w_key, w_value, w_out, doc_ids):
    bf16, f32 = jnp.bfloat16, jnp.float32
    vmem, dma = pltpu.VMEM, pltpu.SemaphoreType.DMA
    scratch = [
        vmem((HALO + ROWS, D), bf16),
        vmem((D, ROWS), bf16),
        vmem((4, D), f32),
        vmem((CHIP, D), bf16),
        vmem((2, 2 * CHUNKS, D, 128), bf16),
        vmem((4, 128, 128), f32),
        vmem((CHIP, 128), f32),
        vmem((CHIP, 128), f32),
        vmem((8, 128), jnp.int32),
        vmem((8, 128), jnp.int32),
        vmem((16, 128), f32),
        vmem((NB, 128, 256), f32),
        vmem((2, 2, 2, CHIP, 128), bf16),
        vmem((2, 4, CHIP + WINDOW, 128), bf16),
        vmem((2, 4, CHIP + WINDOW, 128), bf16),
        vmem((2, 2, WINDOW, 128), bf16),
        vmem((2, 2, WINDOW, 128), bf16),
        vmem((2, CHIP, 512), bf16),
        vmem((2, D, ROWS), f32),
        vmem((D, ROWS), bf16),
        vmem((D, ROWS), bf16),
        dma((14,)),
        dma((2, CHUNKS, 8)),
        dma((2, CHUNKS, 8)),
        dma((NCB,)),
        dma((NCB,)),
        dma((2,)),
        dma((2,)),
        dma((2, 2)),
        dma((2, 2)),
        dma((4,)),
        dma((4,)),
        dma((4,)),
    ]
    hbm = pl.BlockSpec(memory_space=pl.ANY)
    out = pl.pallas_call(
        kernel,
        out_shape=jax.ShapeDtypeStruct((D, ROWS), bf16),
        in_specs=[hbm, pl.BlockSpec(memory_space=pltpu.VMEM), *[hbm] * 7],
        out_specs=hbm,
        scratch_shapes=scratch,
        compiler_params=pltpu.CompilerParams(
            collective_id=0, has_side_effects=True, vmem_limit_bytes=67043328
        ),
        name="attention_block",
    )(
        hidden_in.T, norm_gain, conv_weight, w_query, w_key, w_value, w_out.T,
        doc_ids.reshape(16, 128), jnp.asarray(rope_tables()),
    )
    return out.T


def solution(mesh):
    in_specs = (
        P(("dp", "seq", "tensor"), None),
        P(),
        P(),
        P(None, "tensor"),
        P(None, "tensor"),
        P(None, "tensor"),
        P("tensor", None),
        P(("dp", "seq")),
    )
    out_specs = P(("dp", "seq", "tensor"), None)
    return jax.shard_map(local, mesh=mesh, in_specs=in_specs, out_specs=out_specs, check_vma=False)
```

time: 89.5 us -> 74.1 us (0.83)
  local copies, waits for them, and re-layouts: 13.6 us -> 3.62 us
  Pallas kernels: 75.3 us -> 70.3 us
    pallas_call x1, Pallas kernels: 75.3 us -> 70.3 us  [local(): pl.pallas_call(kernel, out_shape=jax.ShapeDtypeStruct((D, ROWS), bf16), i...]
    pallas_call x1 -> x0, local copies, waits for them, and re-layouts: 4.57 us -> none  [local(): pl.pallas_call(kernel, out_shape=jax.ShapeDtypeStruct((ROWS, D), bf16), i...]
    unnamed x4 -> x1, local copies, waits for them, and re-layouts: 7.73 us -> 3.62 us
    reshape x1 -> x0, local copies, waits for them, and re-layouts: 1.31 us -> none  [local(): norm_gain.reshape(1, D)]
where the time goes in v2:
time: 74.1 us; the launch traced here: 73.9 us
  Pallas kernels  70.3 us (95%)
  local copies, waits for them, and re-layouts  3.62 us (5%)
    pallas_call x1, Pallas kernels, local(): pl.pallas_call(kernel, out_shape=jax.ShapeDtypeStruct((D, ROWS), bf16), i...  70.3 us
    unnamed x1, local copies, waits for them, and re-layouts  3.62 us

profile of v2, /device:TPU:1, one launch (start us, length us, event | category | flops | bytes accessed | tf_op | source)
XLA Modules:
  0.0 73.9 jit_solution(1346726284447194049)
XLA Ops:
  0.0 70.3 %attention_block.1 = bf16[2880,512]{1,0:T(8,128)(2,1)} custom-call(bf16[2880,512]{1,0:T(8,128)(2,1)} %bitcast.5, f32[2880]{0:T(1024)} %gain.1, f32[4,2880]{1,0:T(4,128)} %conv_h.1, bf16[2880,512]{1,0:T(8,128)(2,1)} %wq_h.1, bf16[2880,128]{1,0:T(8,128)(2,1)} %wk_h.1, bf16[2880,128]{1,0:T(8,128)(2,1)} %wv_h.1, bf16[2880,512]{1,0:T(8,128)(2,1)} %bitcast.6, ...), custom_call_target="tpu_custom_call" | custom-call | tf_op jit(solution)/shard_map/attention_block/pallas_call | solution.py:521
  70.3 3.6 %copy.11 = bf16[512,2880]{0,1:T(8,128)(2,1)} copy(bf16[512,2880]{0,1:T(8,128)(2,1)} %bitcast.4) | data formatting | bytes 5898240

commit v3 on v2

--- a/solution.py
+++ b/solution.py
@@ -26,23 +26,24 @@
 NCB = ROWS // CB
 PIECE = D // 8
 CHUNKS = 5
-SLOTS = (
-    ((0, 0),),
-    ((0, 1), (1, 0)),
-    ((0, 2),),
-    ((2, 0), (1, 1)),
-    ((0, 3),),
-    ((2, 1), (1, 2)),
-    ((0, 4),),
-    ((2, 2), (1, 3)),
-    (),
-    ((2, 3),),
-    ((1, 4),),
-    ((2, 4),),
-    (),
-    (),
-    (),
-)
+BEFORE = {
+    "kv1": ((5, 1, 0),),
+    "q10": ((5, 0, 1), (5, 1, 1)),
+    "q11": ((5, 1, 2),),
+}
+AFTER = {
+    "norm": {7: ((0, 0, 0),)},
+    "kv0": {1: ((0, 1, 0),), 2: ((0, 0, 1),)},
+    "q0": {1: ((1, 0, 0), (2, 0, 0)), 2: ((0, 1, 1),), 3: ((1, 1, 0), (2, 1, 0)), 4: ((0, 0, 2), (2, 0, 1))},
+    "own": {1: ((1, 0, 1),), 2: ((3, 0, 0), (4, 0, 0), (0, 1, 2)), 3: ((1, 1, 1), (2, 1, 1)), 4: ((0, 0, 3),), 5: ((3, 1, 0), (4, 1, 0)), 6: ((1, 0, 2),), 7: ((0, 1, 3), (2, 0, 2))},
+    "of": {1: ((1, 1, 2), (3, 0, 1)), 2: ((0, 0, 4),), 3: ((5, 0, 0), (3, 1, 1), (2, 1, 2), (1, 0, 3)), 4: ((4, 0, 1), (0, 1, 4))},
+    "kv1": {1: ((4, 1, 1), (1, 1, 3)), 2: ((2, 0, 3),)},
+    "q10": {1: ((3, 0, 2), (3, 1, 2), (4, 0, 2), (4, 1, 2), (2, 1, 3), (1, 0, 4), (1, 1, 4)), 2: ((2, 0, 4),)},
+    "ar0": {2: ((3, 0, 3),), 4: ((4, 0, 3),), 6: ((5, 0, 2), (3, 1, 3), (2, 1, 4))},
+    "q11": {2: ((4, 1, 3), (3, 0, 4), (3, 1, 4), (4, 0, 4))},
+    "ao0": {1: ((5, 0, 3),)},
+    "ar1": {2: ((5, 1, 3), (4, 1, 4)), 8: ((5, 0, 4), (5, 1, 4))},
+}
 A, B, AL, AR, BL, BR, ALL_, BRR = range(8)
 
 
@@ -56,10 +57,10 @@
 
 
 def kernel(
-    hid_h, gain, conv_h, wq_h, wk_h, wv_h, wo_h, doc_h, rope_h, out_h,
+    hid_h, gain, conv_h, wq_h, wk_h, wv_h, wo_h, doc_h, rope_h, outv,
     hid, flat, conv, mixed, w, rope, cosv, sinv, doc, dprev, docx, bias,
-    q, kx, vx, tail, halo, att, acc, psend, precv,
-    load_sem, wsem_s, wsem_r, mix_s, mix_r, edge_s, edge_r, kv_s, kv_r, part_s, part_r, out_sem,
+    q, kx, vx, tail, halo, att, att2, w2, acc,
+    load_sem, wsem_s, wsem_r, mix_s, mix_r, edge_s, edge_r, kv_s, kv_r, far_s, far_r, att_s, att_r,
 ):
     dp, seq, tensor = lax.axis_index("dp"), lax.axis_index("seq"), lax.axis_index("tensor")
     yh, core = tensor // 2, tensor % 2
@@ -127,16 +128,88 @@
         ref = wq_h if c < 3 else wo_h
         return ref.at[span(at, l), pl.ds((((c - 1) % 2) * 2 + s) * 128, 128)]
 
-    sent = []
-
-    def send(s, c, kind, src, dst, device):
-        copy = remote(src, dst, wsem_s.at[s, c, kind], wsem_r.at[s, c, kind], device)
-        copy.start()
-        sent.append(copy)
-
-    def arrived(s, c, kind, at, l):
+    def before(s):
+        return (ring[s] + 3) % 4
+
+    def after(s):
+        return (ring[s] + 1) % 4
+
+    def over(s):
+        return (ring[s] + 2) % 4
+
+    def sends(s, c):
+        mine, given = piece(s, c, ring[s], yl), piece(s, c, ring[s], 1 - yl)
+        from_left, from_right = piece(s, c, before(s), yl), piece(s, c, after(s), 1 - yl)
+        return {
+            A: (source(s, c, ring[s], 1 - yl), given, cross),
+            B: (mine, mine, ylo),
+            AL: (mine, mine, right[s]),
+            AR: (mine, mine, left[s]),
+            BL: (given, given, right[s]),
+            BR: (given, given, left[s]),
+            ALL_: (from_left, from_left, right[s]),
+            BRR: (from_right, from_right, left[s]),
+        }
+
+    def sending(s, c, kind):
+        src, dst, device = sends(s, c)[kind]
+        return remote(src, dst, wsem_s.at[s, c, kind], wsem_r.at[s, c, kind], device)
+
+    def arrived(s, c, kind):
+        at, l = {
+            A: (ring[s], yl), B: (ring[s], 1 - yl), AL: (before(s), yl), AR: (after(s), yl),
+            BL: (before(s), 1 - yl), BR: (after(s), 1 - yl), ALL_: (over(s), yl), BRR: (over(s), 1 - yl),
+        }[kind]
         ref = piece(s, c, at, l)
         remote(ref, ref, wsem_s.at[s, c, kind], wsem_r.at[s, c, kind], cross).wait_recv()
+
+    def far_copy(s, c, k):
+        at = (ring[s], before(s), after(s), over(s))[k]
+        rows = pl.ds(pl.multiple_of(at * (2 * PIECE), 16), 2 * PIECE)
+        sems = far_s.at[s, c - 2, k], far_r.at[s, c - 2, k]
+        return remote(w.at[1, s * CHUNKS + c, rows], w2.at[1, (c - 3) * 2 + s, rows], *sems, partner)
+
+    stages = (
+        ((A,), (AL, AR, B), ()),
+        ((B,), (BR, BL), (0,)),
+        ((AL,), (ALL_,), ()),
+        ((BR,), (BRR,), ()),
+        ((AR, BL), (), (1, 2)),
+        ((ALL_, BRR), (), (3,)),
+    )
+
+    def run(steps):
+        for stage, s, c in steps:
+            awaited, forwarded, complete = stages[stage]
+            for kind in awaited:
+                arrived(s, c, kind)
+            for kind in forwarded:
+                sending(s, c, kind).start()
+            if c >= 3:
+                for k in complete:
+                    far_copy(s, c, k).start()
+
+    zero = core // 2
+
+    def phase(name, low, high, body, hooks=()):
+        run(BEFORE.get(name, ()))
+
+        def step(i, carry):
+            body(i)
+            return carry
+
+        at, hooks, steps = low, dict(hooks), AFTER.get(name, {})
+        for count in sorted({*hooks, *steps}):
+            lax.fori_loop(at + zero, low + count, step, 0)
+            hooks.get(count, lambda: None)()
+            run(steps.get(count, ()))
+            at = low + count
+        if at < high:
+            lax.fori_loop(at, high, step, 0)
+
+    def wo_copy(j):
+        src = wo_h.at[:, pl.ds(j * 128, 128)]
+        return remote(src, w2.at[0, j], far_s.at[j // 2, 0, j % 2], far_r.at[j // 2, 0, j % 2], partner)
 
     def before(s):
         return (ring[s] + 3) % 4
@@ -178,11 +251,10 @@
             arrived(s, c, ALL_, over(s), yl)
             arrived(s, c, BRR, over(s), 1 - yl)
 
-    stages = (s0, s1, s2)
-
-    def slot(i):
-        for stage, c in SLOTS[i]:
-            stages[stage](c)
+    def far_arrived(c):
+        for s in range(2):
+            for k in range(4):
+                far_copy(s, c, k).wait_recv()
 
     edge = [
         remote(hid.at[pl.ds(HALO + ROWS - 8, 8)], hid.at[pl.ds(8, 8)], edge_s.at[0], edge_r.at[0], next_dev),
@@ -190,7 +262,7 @@
     ]
     for c in range(CHUNKS):
         for s in range(2):
-            send(s, c, A, source(s, c, ring[s], 1 - yl), piece(s, c, ring[s], 1 - yl), cross)
+            sending(s, c, A).start()
     edge[1].start()
 
     for i in range(2):
@@ -240,15 +312,17 @@
         rows = pl.ds(pl.multiple_of(start + b * CB, CB), CB)
         return remote(mixed.at[rows], mixed.at[rows], mix_s.at[b], mix_r.at[b], partner)
 
-    def norm_step(b, carry):
+    def norm_step(i):
+        b = (i + 1) % NCB
+
+        @pl.when(i == NCB - 1)
+        def _():
+            edge[0].wait()
+
         norm_conv(b)
         mix_copy(b, own).start()
-        return carry
-
-    lax.fori_loop(1, NCB, norm_step, 0)
-    edge[0].wait()
-    norm_step(0, 0)
-    slot(0)
+
+    phase("norm", 0, NCB, norm_step)
 
     loads[2].wait()
     loads[3].wait()
@@ -258,7 +332,7 @@
     docx[0:1, :] = jnp.where(place == 0, -1.0, dprev[7:8, :].astype(jnp.float32))
     docx[1:9, :] = doc[...].astype(jnp.float32)
 
-    def table_step(b, carry):
+    def table_step(b):
         rows = pl.ds(pl.multiple_of(b * WINDOW, WINDOW), WINDOW)
         cb = rope[2, pl.ds(place * NB + b, 1), :]
         sb = rope[3, pl.ds(place * NB + b, 1), :]
@@ -271,9 +345,9 @@
         mine = jnp.sum(jnp.where(r == c, k1, 0.0), axis=1, keepdims=True)
         bias[b, :, 0:128] = jnp.where(jnp.logical_and(c > r, k0 == mine), 0.0, NEG)
         bias[b, :, 128:256] = jnp.where(jnp.logical_and(c <= r, k1 == mine), 0.0, NEG)
-        return carry
-
-    lax.fori_loop(0, NB, table_step, 0)
+
+    lax.fori_loop(0, NB, lambda b, carry: table_step(b), None)
+    run(AFTER.get("table", {}).get(1, ()))
 
     def spread(dst, g, rows, v):
         low = lax.broadcasted_iota(jnp.int32, v.shape, 1) < 64
@@ -310,21 +384,16 @@
             v = turn(p[:, i * 128:(i + 1) * 128], rows) * 0.125
             q[g, j, i, rows, :] = v.astype(jnp.bfloat16)
 
-    def kv_range(g):
-        def step(i, carry):
-            project_kv(g, pl.multiple_of(i * ROWS, ROWS))
-            return carry
-
-        lax.fori_loop(0, 2, step, 0)
+    def kv_phase(name, g):
+        phase(name, 0, 2, lambda i: project_kv(g, pl.multiple_of(i * ROWS, ROWS)))
         for i in range(2):
             kv_copy(g, i).start()
 
-    def q_range(g, low, high):
-        def step(i, carry):
-            project_q(g, i // 2, pl.multiple_of((i % 2) * ROWS, ROWS))
-            return carry
-
-        lax.fori_loop(low, high, step, 0)
+    def q_phase(name, g, low, high):
+        phase(
+            name, low, high,
+            lambda i: project_q(g, i // 2, pl.multiple_of((i % 2) * ROWS, ROWS)),
+        )
 
     def kv_copy(g, i):
         return remote(
@@ -350,16 +419,22 @@
             weights.append(e.astype(jnp.bfloat16))
         o = jnp.dot(jnp.concatenate(weights, axis=1), v2, preferred_element_type=jnp.float32)
         o = (o * jnp.where(low, inverse[0], inverse[1])).astype(jnp.bfloat16)
-        att[g, rows, j * 256:j * 256 + 128] = o[0:128]
-        att[g, rows, j * 256 + 128:j * 256 + 256] = o[128:256]
-
-    def attend_blocks(g, heads, low, high):
-        def step(b, carry):
+        att[g, j, rows, 0:128] = o[0:128]
+        att[g, j, rows, 128:256] = o[128:256]
+
+    def attend_phase(name, g, heads, low, high, sent):
+        count = high - low
+
+        def body(i):
+            b = low + (i + (count // 2) * (1 - core)) % count
             for j in heads:
                 attend(g, j, b)
-            return carry
-
-        lax.fori_loop(low, high, step, 0)
+
+        def leave():
+            for j in heads:
+                att_copy(sent, j).start()
+
+        phase(name, 0, count, body, {min(4, count): leave})
 
     def halo_in(g):
         for i in range(2):
@@ -370,113 +445,99 @@
         spread(kx, g, pl.ds(0, WINDOW), halo[g, 0].astype(jnp.float32))
         spread(vx, g, pl.ds(0, WINDOW), halo[g, 1].astype(jnp.float32))
 
-    def out_product(g, blocks, features, start):
-        weights = jnp.concatenate([w[g, b, features, :] for b, _ in blocks], axis=1)
-        low, high = blocks[0][1] * 128, blocks[-1][1] * 128 + 128
+    def att_copy(k, j):
+        g = k // 2
+        start, count = ((128, ROWS - 128), (0, 128), (0, ROWS))[k]
+        rows = pl.ds(pl.multiple_of(other + start, 128), count)
+        dst = att2.at[g, j, pl.ds(start, count)]
+        return remote(att.at[g, j, rows], dst, att_s.at[k, j], att_r.at[k, j], partner)
+
+    def out_product(units, features, start, count):
+        weights, heads = [], []
+        rows = pl.ds(pl.multiple_of(own + start, 128), count)
+        for g, j in units:
+            weights += [w[g, 3 + j, features, :], w[g, CHUNKS + 3 + j, features, :]]
+            weights += [w2[g, 2 * j, features, :], w2[g, 2 * j + 1, features, :]]
+            heads += [att[g, j, rows, :], att2[g, j, start:start + count, :]]
         return lax.dot_general(
-            weights, att[g, pl.ds(start, ROWS), low:high], (((1,), (1,)), ((), ())),
-            preferred_element_type=jnp.float32,
+            jnp.concatenate(weights, axis=1), jnp.concatenate(heads, axis=1),
+            (((1,), (1,)), ((), ())), preferred_element_type=jnp.float32,
         )
 
     def feature_rows(i):
         return pl.ds(pl.multiple_of(i * FC, 8), FC)
 
-    both_parts = ((3, 0), (CHUNKS + 3, 1), (4, 2), (CHUNKS + 4, 3))
-
-    def out_own(h):
-        def step(i, carry):
-            acc[h, feature_rows(i), :] = out_product(0, both_parts, feature_rows(i), h * ROWS)
-            return carry
-
-        lax.fori_loop(0, 4, step, 0)
-
-    def out_add():
-        def step(i, carry):
-            for h in range(2):
-                acc[h, feature_rows(i), :] += out_product(1, both_parts[:2], feature_rows(i), h * ROWS)
-            return carry
-
-        lax.fori_loop(0, 4, step, 0)
-
-    def part_copy(i):
+    near = ((0, 0), (0, 1))
+
+    def out_near(i):
         rows = feature_rows(i)
-        return remote(psend.at[rows], precv.at[rows], part_s.at[i], part_r.at[i], partner)
-
-    def out_copy(i):
+        acc[rows, 128:ROWS] = out_product(near, rows, 128, ROWS - 128)
+
+    def out_first(i):
         rows = feature_rows(i)
-        return pltpu.make_async_copy(flat.at[rows], out_h.at[rows], out_sem.at[i])
-
-    def far_step(i, carry):
+        acc[rows, 0:128] = out_product(near, rows, 0, 128)
+
+    def out_next(i):
         rows = feature_rows(i)
-        p = acc[1 - core, rows, :] + out_product(1, both_parts[2:], rows, other)
-        psend[rows, :] = p.astype(jnp.bfloat16)
-        part_copy(i).start()
-        return carry
-
-    def near_step(i, carry):
+        acc[rows, :] += out_product(((1, 0),), rows, 0, ROWS)
+
+    def out_last(i):
         rows = feature_rows(i)
-        p = acc[core, rows, :] + out_product(1, both_parts[2:], rows, own)
-        part_copy(i).wait_recv()
-        p = p + precv[rows, :].astype(jnp.float32)
-        flat[rows, :] = (flat[rows, :].astype(jnp.float32) + p).astype(jnp.bfloat16)
-        out_copy(i).start()
-        return carry
+        p = acc[rows, :] + out_product(((1, 1),), rows, 0, ROWS)
+        outv[rows, :] = (flat[rows, :].astype(jnp.float32) + p).astype(jnp.bfloat16)
 
     for i in range(4, 10):
         loads[i].wait()
     for b in range(NCB):
         mix_copy(b, other).wait_recv()
-    kv_range(0)
-    slot(1)
-    q_range(0, 0, 2)
-    slot(2)
-    q_range(0, 2, 4)
-    slot(3)
-    attend_blocks(0, (0, 1), 1, 3)
-    slot(4)
-    attend_blocks(0, (0, 1), 3, 6)
-    slot(5)
-    attend_blocks(0, (0, 1), 6, 8)
-    slot(6)
+    for j in range(4):
+        wo_copy(j).start()
+    kv_phase("kv0", 0)
+    q_phase("q0", 0, 0, 4)
+    attend_phase("own", 0, (0, 1), 1, NB, 0)
     for i in range(10, 14):
         loads[i].wait()
-    out_own(1)
-    slot(7)
-    s3(0)
-    kv_range(1)
-    slot(8)
-    s3(1)
-    q_range(1, 0, 2)
-    slot(9)
+    for j in range(4):
+        wo_copy(j).wait_recv()
+    for j in range(2):
+        att_copy(0, j).wait_recv()
+    phase("of", 0, 4, out_near)
+    kv_phase("kv1", 1)
+    q_phase("q10", 1, 0, 2)
     halo_in(1)
-    attend_blocks(1, (0,), 0, NB)
-    slot(10)
+    attend_phase("ar0", 1, (0,), 0, NB, 2)
+    q_phase("q11", 1, 2, 4)
     halo_in(0)
-    attend_blocks(0, (0, 1), 0, 1)
-    out_own(0)
-    slot(11)
-    s3(2)
-    q_range(1, 2, 4)
-    slot(12)
-    attend_blocks(1, (1,), 0, NB)
-    slot(13)
-    s3(3)
-    out_add()
-    slot(14)
-    s3(4)
-    lax.fori_loop(0, 4, far_step, 0)
-    lax.fori_loop(0, 4, near_step, 0)
-
-    for i in range(4):
-        out_copy(i).wait()
-        part_copy(i).wait_send()
+    attend_phase("ao0", 0, (0, 1), 0, 1, 1)
+    attend_phase("ar1", 1, (1,), 0, NB, 2)
+    for j in range(2):
+        att_copy(1, j).wait_recv()
+    phase("of2", 0, 4, out_first)
+    run(BEFORE.get("on", ()))
+    far_arrived(3)
+    att_copy(2, 0).wait_recv()
+    lax.fori_loop(0, 4, lambda i, carry: out_next(i), None)
+    run(BEFORE.get("ol", ()))
+    far_arrived(4)
+    att_copy(2, 1).wait_recv()
+    lax.fori_loop(0, 4, lambda i, carry: out_last(i), None)
+
     for b in range(NCB):
         mix_copy(b, own).wait_send()
-    for g in range(2):
-        for i in range(2):
+    for j in range(4):
+        wo_copy(j).wait_send()
+    for i in range(2):
+        for g in range(2):
             kv_copy(g, i).wait_send()
-    for copy in sent:
-        copy.wait_send()
+        for k in range(3):
+            att_copy(k, i).wait_send()
+    for s in range(2):
+        for c in range(CHUNKS):
+            for kind in range(8):
+                sending(s, c, kind).wait_send()
+            if c >= 3:
+                for k in range(4):
+                    far_copy(s, c, k).wait_send()
 
 
 def local(hidden_in, norm_gain, conv_weight, w_query, w_key, w_value, w_out, doc_ids):
@@ -500,10 +561,10 @@
         vmem((2, 4, CHIP + WINDOW, 128), bf16),
         vmem((2, 2, WINDOW, 128), bf16),
         vmem((2, 2, WINDOW, 128), bf16),
-        vmem((2, CHIP, 512), bf16),
-        vmem((2, D, ROWS), f32),
-        vmem((D, ROWS), bf16),
-        vmem((D, ROWS), bf16),
+        vmem((2, 2, CHIP, 256), bf16),
+        vmem((2, 2, ROWS, 256), bf16),
+        vmem((2, 4, D, 128), bf16),
+        vmem((D, ROWS), f32),
         dma((14,)),
         dma((2, CHUNKS, 8)),
         dma((2, CHUNKS, 8)),
@@ -513,19 +574,20 @@
         dma((2,)),
         dma((2, 2)),
         dma((2, 2)),
-        dma((4,)),
-        dma((4,)),
-        dma((4,)),
+        dma((2, 3, 4)),
+        dma((2, 3, 4)),
+        dma((3, 2)),
+        dma((3, 2)),
     ]
     hbm = pl.BlockSpec(memory_space=pl.ANY)
     out = pl.pallas_call(
         kernel,
-        out_shape=jax.ShapeDtypeStruct((D, ROWS), bf16),
+        out_shape=pltpu.VMEM((D, ROWS), bf16),
         in_specs=[hbm, pl.BlockSpec(memory_space=pltpu.VMEM), *[hbm] * 7],
-        out_specs=hbm,
+        out_specs=pl.BlockSpec(memory_space=pltpu.VMEM),
         scratch_shapes=scratch,
         compiler_params=pltpu.CompilerParams(
-            collective_id=0, has_side_effects=True, vmem_limit_bytes=67043328
+            collective_id=0, has_side_effects=True, vmem_limit_bytes=60 << 20
         ),
         name="attention_block",
     )(

time: 74.1 us -> 64.2 us (0.87)
  Pallas kernels: 70.3 us -> 62.5 us
  local copies, waits for them, and re-layouts: 3.62 us -> 1.6 us
    pallas_call x1, Pallas kernels: 70.3 us -> 62.5 us  [local(): pl.pallas_call(kernel, out_shape=pltpu.VMEM((D, ROWS), bf16), in_specs=[h...]
    unnamed x1, local copies, waits for them, and re-layouts: 3.62 us -> 1.6 us
where the time goes in v3:
time: 64.2 us; the launch traced here: 64.1 us
  Pallas kernels  62.5 us (97%)
  local copies, waits for them, and re-layouts  1.6 us (2%)
    pallas_call x1, Pallas kernels, local(): pl.pallas_call(kernel, out_shape=pltpu.VMEM((D, ROWS), bf16), in_specs=[h...  62.5 us
    unnamed x1, local copies, waits for them, and re-layouts  1.6 us

profile of v3, /device:TPU:1, one launch (start us, length us, event | category | flops | bytes accessed | tf_op | source)
XLA Modules:
  0.0 64.1 jit_solution(14712648714697419851)
XLA Ops:
  0.0 62.5 %attention_block.1 = bf16[2880,512]{1,0:T(8,128)(2,1)S(1)} custom-call(bf16[2880,512]{1,0:T(8,128)(2,1)} %bitcast.5, f32[2880]{0:T(1024)} %gain.1, f32[4,2880]{1,0:T(4,128)} %conv_h.1, bf16[2880,512]{1,0:T(8,128)(2,1)} %wq_h.1, bf16[2880,128]{1,0:T(8,128)(2,1)} %wk_h.1, bf16[2880,128]{1,0:T(8,128)(2,1)} %wv_h.1, bf16[2880,512]{1,0:T(8,128)(2,1)} %bitcast.6, ...), custom_call_target="tpu_custom_call" | custom-call | tf_op jit(solution)/shard_map/attention_block/pallas_call | solution.py:583
  62.5 1.6 %copy.11 = bf16[512,2880]{0,1:T(8,128)(2,1)} copy(bf16[512,2880]{0,1:T(8,128)(2,1)S(1)} %bitcast.4) | data formatting | bytes 5898240

commit v4 on v3

--- a/solution.py
+++ b/solution.py
@@ -24,6 +24,7 @@
 FC = D // 4
 CB = 64
 NCB = ROWS // CB
+UNITS = 2
 PIECE = D // 8
 CHUNKS = 5
 BEFORE = {
@@ -34,15 +35,14 @@
 AFTER = {
     "norm": {7: ((0, 0, 0),)},
     "kv0": {1: ((0, 1, 0),), 2: ((0, 0, 1),)},
-    "q0": {1: ((1, 0, 0), (2, 0, 0)), 2: ((0, 1, 1),), 3: ((1, 1, 0), (2, 1, 0)), 4: ((0, 0, 2), (2, 0, 1))},
-    "own": {1: ((1, 0, 1),), 2: ((3, 0, 0), (4, 0, 0), (0, 1, 2)), 3: ((1, 1, 1), (2, 1, 1)), 4: ((0, 0, 3),), 5: ((3, 1, 0), (4, 1, 0)), 6: ((1, 0, 2),), 7: ((0, 1, 3), (2, 0, 2))},
-    "of": {1: ((1, 1, 2), (3, 0, 1)), 2: ((0, 0, 4),), 3: ((5, 0, 0), (3, 1, 1), (2, 1, 2), (1, 0, 3)), 4: ((4, 0, 1), (0, 1, 4))},
-    "kv1": {1: ((4, 1, 1), (1, 1, 3)), 2: ((2, 0, 3),)},
-    "q10": {1: ((3, 0, 2), (3, 1, 2), (4, 0, 2), (4, 1, 2), (2, 1, 3), (1, 0, 4), (1, 1, 4)), 2: ((2, 0, 4),)},
-    "ar0": {2: ((3, 0, 3),), 4: ((4, 0, 3),), 6: ((5, 0, 2), (3, 1, 3), (2, 1, 4))},
-    "q11": {2: ((4, 1, 3), (3, 0, 4), (3, 1, 4), (4, 0, 4))},
-    "ao0": {1: ((5, 0, 3),)},
-    "ar1": {2: ((5, 1, 3), (4, 1, 4)), 8: ((5, 0, 4), (5, 1, 4))},
+    "q0": {1: ((1, 0, 0), (2, 0, 0)), 2: ((0, 1, 1),), 3: ((1, 1, 0), (2, 1, 0), (0, 0, 2)), 4: ((1, 0, 1), (2, 0, 1))},
+    "own": {1: ((0, 1, 2),), 2: ((3, 0, 0), (4, 0, 0)), 3: ((1, 1, 1), (2, 1, 1)), 4: ((0, 0, 3),), 6: ((3, 1, 0), (4, 1, 0), (1, 0, 2)), 7: ((0, 1, 3),)},
+    "of": {1: ((1, 1, 2), (3, 0, 1), (2, 0, 2)), 2: ((0, 0, 4),), 3: ((5, 0, 0), (3, 1, 1), (4, 0, 1), (2, 1, 2), (1, 0, 3)), 4: ((0, 1, 4),)},
+    "kv1": {1: ((4, 1, 1), (1, 1, 3)), 2: ((3, 0, 2), (2, 0, 3))},
+    "q10": {1: ((3, 1, 2), (4, 0, 2), (4, 1, 2), (2, 1, 3), (1, 0, 4), (1, 1, 4)), 2: ((3, 0, 3), (2, 0, 4))},
+    "ar0": {2: ((5, 0, 2), (4, 0, 3)), 4: ((3, 1, 3), (2, 1, 4))},
+    "q11": {2: ((4, 1, 3), (5, 0, 3), (3, 0, 4), (3, 1, 4), (4, 0, 4))},
+    "ar1": {2: ((5, 1, 3), (4, 1, 4)), 4: ((5, 0, 4), (5, 1, 4))},
 }
 A, B, AL, AR, BL, BR, ALL_, BRR = range(8)
 
@@ -374,8 +374,8 @@
         v = p[:, 128:256]
         spread(kx, g, ext, k)
         spread(vx, g, ext, v)
-        tail[g, 0, :, :] = k[ROWS - WINDOW:].astype(jnp.bfloat16)
-        tail[g, 1, :, :] = v[ROWS - WINDOW:].astype(jnp.bfloat16)
+        tail[start // ROWS, g, 0] = k[ROWS - WINDOW:].astype(jnp.bfloat16)
+        tail[start // ROWS, g, 1] = v[ROWS - WINDOW:].astype(jnp.bfloat16)
 
     def project_q(g, j, start):
         rows = pl.ds(start, ROWS)
@@ -384,8 +384,11 @@
             v = turn(p[:, i * 128:(i + 1) * 128], rows) * 0.125
             q[g, j, i, rows, :] = v.astype(jnp.bfloat16)
 
-    def kv_phase(name, g):
-        phase(name, 0, 2, lambda i: project_kv(g, pl.multiple_of(i * ROWS, ROWS)))
+    def kv_phase(name, g, hooks=()):
+        def body(i):
+            project_kv(g, pl.multiple_of(((core + i) % 2) * ROWS, ROWS))
+
+        phase(name, 0, 2, body, hooks)
         for i in range(2):
             kv_copy(g, i).start()
 
@@ -397,44 +400,56 @@
 
     def kv_copy(g, i):
         return remote(
-            tail.at[g, i], halo.at[1 - g, i],
+            tail.at[1, g, i], halo.at[1 - g, i],
             kv_s.at[g, i], kv_r.at[1 - g, i], next_chip,
         )
 
-    def attend(g, j, b):
-        rows = pl.ds(pl.multiple_of(b * WINDOW, WINDOW), WINDOW)
-        keys = pl.ds(pl.multiple_of(b * WINDOW, WINDOW), 2 * WINDOW)
-        extra = bias[b]
-        extra = jnp.concatenate([extra, extra], axis=0)
-        low = lax.broadcasted_iota(jnp.int32, (256, 128), 1) < 64
-        both = jnp.concatenate([q[g, j, 0, rows, :], q[g, j, 1, rows, :]], axis=0)
-        k2 = jnp.concatenate([kx[g, 2 * j, keys, :], kx[g, 2 * j + 1, keys, :]], axis=0)
-        v2 = jnp.concatenate([vx[g, 2 * j, keys, :], vx[g, 2 * j + 1, keys, :]], axis=0)
-        s = lax.dot_general(both, k2, (((1,), (1,)), ((), ())), preferred_element_type=jnp.float32)
-        weights, inverse = [], []
-        for i in range(2):
-            half = s[:, i * 256:(i + 1) * 256] + extra
-            e = jnp.exp(half - jnp.max(half, axis=1, keepdims=True))
-            inverse.append(1.0 / jnp.sum(e, axis=1, keepdims=True))
-            weights.append(e.astype(jnp.bfloat16))
-        o = jnp.dot(jnp.concatenate(weights, axis=1), v2, preferred_element_type=jnp.float32)
-        o = (o * jnp.where(low, inverse[0], inverse[1])).astype(jnp.bfloat16)
-        att[g, j, rows, 0:128] = o[0:128]
-        att[g, j, rows, 128:256] = o[128:256]
+    def attend(units):
+        ones = lax.broadcasted_iota(jnp.int32, (512, 128), 0) // 256
+        ones = ones == lax.broadcasted_iota(jnp.int32, (512, 128), 1) // 64
+        ones = jnp.where(ones, 1.0, 0.0).astype(jnp.bfloat16)
+        scores, weights = [], []
+        for g, j, b in units:
+            rows = pl.ds(pl.multiple_of(b * WINDOW, WINDOW), WINDOW)
+            keys = pl.ds(pl.multiple_of(b * WINDOW, WINDOW), 2 * WINDOW)
+            both = jnp.concatenate([q[g, j, 0, rows, :], q[g, j, 1, rows, :]], axis=0)
+            k2 = jnp.concatenate([kx[g, 2 * j, keys, :], kx[g, 2 * j + 1, keys, :]], axis=0)
+            scores.append(
+                lax.dot_general(both, k2, (((1,), (1,)), ((), ())), preferred_element_type=jnp.float32)
+            )
+        for (g, j, b), s in zip(units, scores):
+            extra = bias[b]
+            extra = jnp.concatenate([extra, extra], axis=0)
+            parts = []
+            for i in range(2):
+                half = s[:, i * 256:(i + 1) * 256] + extra
+                e = jnp.exp(half - jnp.max(half, axis=1, keepdims=True))
+                parts.append(e.astype(jnp.bfloat16))
+            weights.append(jnp.concatenate(parts, axis=1))
+        for (g, j, b), p in zip(units, weights):
+            rows = pl.ds(pl.multiple_of(b * WINDOW, WINDOW), WINDOW)
+            keys = pl.ds(pl.multiple_of(b * WINDOW, WINDOW), 2 * WINDOW)
+            v2 = jnp.concatenate([vx[g, 2 * j, keys, :], vx[g, 2 * j + 1, keys, :]], axis=0)
+            v2 = jnp.concatenate([v2, ones], axis=1)
+            o = jnp.dot(p, v2, preferred_element_type=jnp.float32)
+            o = (o[:, 0:128] / o[:, 128:256]).astype(jnp.bfloat16)
+            att[g, j, rows, 0:128] = o[0:128]
+            att[g, j, rows, 128:256] = o[128:256]
 
     def attend_phase(name, g, heads, low, high, sent):
         count = high - low
+        rounds = count * len(heads) // UNITS if count > 1 else 1
 
         def body(i):
-            b = low + (i + (count // 2) * (1 - core)) % count
-            for j in heads:
-                attend(g, j, b)
+            each = 1 if count == 1 else UNITS // len(heads)
+            blocks = [low + (i * each + n + (count // 2) * (1 - core)) % count for n in range(each)]
+            attend([(g, j, b) for b in blocks for j in heads])
 
         def leave():
             for j in heads:
                 att_copy(sent, j).start()
 
-        phase(name, 0, count, body, {min(4, count): leave})
+        phase(name, 0, rounds, body, {(rounds + 1) // 2: leave} if count != 7 else {4: leave})
 
     def halo_in(g):
         for i in range(2):
@@ -477,22 +492,20 @@
         rows = feature_rows(i)
         acc[rows, 0:128] = out_product(near, rows, 0, 128)
 
-    def out_next(i):
-        rows = feature_rows(i)
-        acc[rows, :] += out_product(((1, 0),), rows, 0, ROWS)
-
     def out_last(i):
         rows = feature_rows(i)
-        p = acc[rows, :] + out_product(((1, 1),), rows, 0, ROWS)
+        p = acc[rows, :] + out_product(((1, 0), (1, 1)), rows, 0, ROWS)
         outv[rows, :] = (flat[rows, :].astype(jnp.float32) + p).astype(jnp.bfloat16)
 
     for i in range(4, 10):
         loads[i].wait()
-    for b in range(NCB):
-        mix_copy(b, other).wait_recv()
-    for j in range(4):
-        wo_copy(j).start()
-    kv_phase("kv0", 0)
+    def mixed_in():
+        for b in range(NCB):
+            mix_copy(b, other).wait_recv()
+        for j in range(4):
+            wo_copy(j).start()
+
+    kv_phase("kv0", 0, {1: mixed_in})
     q_phase("q0", 0, 0, 4)
     attend_phase("own", 0, (0, 1), 1, NB, 0)
     for i in range(10, 14):
@@ -516,7 +529,6 @@
     run(BEFORE.get("on", ()))
     far_arrived(3)
     att_copy(2, 0).wait_recv()
-    lax.fori_loop(0, 4, lambda i, carry: out_next(i), None)
     run(BEFORE.get("ol", ()))
     far_arrived(4)
     att_copy(2, 1).wait_recv()
@@ -559,7 +571,7 @@
         vmem((2, 2, 2, CHIP, 128), bf16),
         vmem((2, 4, CHIP + WINDOW, 128), bf16),
         vmem((2, 4, CHIP + WINDOW, 128), bf16),
-        vmem((2, 2, WINDOW, 128), bf16),
+        vmem((2, 2, 2, WINDOW, 128), bf16),
         vmem((2, 2, WINDOW, 128), bf16),
         vmem((2, 2, CHIP, 256), bf16),
         vmem((2, 2, ROWS, 256), bf16),

time: 64.2 us -> 61.5 us (0.958)
  Pallas kernels: 62.5 us -> 59.8 us
    pallas_call x1, Pallas kernels: 62.5 us -> 59.8 us  [local(): pl.pallas_call(kernel, out_shape=pltpu.VMEM((D, ROWS), bf16), in_specs=[h...]
where the time goes in v4:
time: 61.5 us; the launch traced here: 61.4 us
  Pallas kernels  59.8 us (97%)
  local copies, waits for them, and re-layouts  1.6 us (3%)
    pallas_call x1, Pallas kernels, local(): pl.pallas_call(kernel, out_shape=pltpu.VMEM((D, ROWS), bf16), in_specs=[h...  59.8 us
    unnamed x1, local copies, waits for them, and re-layouts  1.6 us

profile of v4, /device:TPU:1, one launch (start us, length us, event | category | flops | bytes accessed | tf_op | source)
XLA Modules:
  0.0 61.4 jit_solution(8200535438070316567)
XLA Ops:
  0.0 59.8 %attention_block.1 = bf16[2880,512]{1,0:T(8,128)(2,1)S(1)} custom-call(bf16[2880,512]{1,0:T(8,128)(2,1)} %bitcast.5, f32[2880]{0:T(1024)} %gain.1, f32[4,2880]{1,0:T(4,128)} %conv_h.1, bf16[2880,512]{1,0:T(8,128)(2,1)} %wq_h.1, bf16[2880,128]{1,0:T(8,128)(2,1)} %wk_h.1, bf16[2880,128]{1,0:T(8,128)(2,1)} %wv_h.1, bf16[2880,512]{1,0:T(8,128)(2,1)} %bitcast.6, ...), custom_call_target="tpu_custom_call" | custom-call | tf_op jit(solution)/shard_map/attention_block/pallas_call | solution.py:595
  59.8 1.6 %copy.11 = bf16[512,2880]{0,1:T(8,128)(2,1)} copy(bf16[512,2880]{0,1:T(8,128)(2,1)S(1)} %bitcast.4) | data formatting | bytes 5898240
